TPU v7x, 32 devices: a 4x4x1 block of a 4x4x8 slice. The times are simulated.
32 devices in a mesh: dp: 1 (over z), tp: 4 (over y), pp: 8 (over x, core).
Axes of the slice: x: 4, y: 4, z: 1, core: 2. Of those that a mesh axis runs over, the one named last changes fastest.
The devices are a block of a 4x4x8 slice.
Arguments:
- x_in: bfloat16 [2, 2, 384, 1024], P(None, 'dp')
- dy_out: bfloat16 [2, 2, 384, 1024], P(None, 'dp')
- w_qkv: bfloat16 [8, 3, 1024, 16, 64], P('pp', None, None, 'tp')
- b_qkv: bfloat16 [8, 3, 16, 64], P('pp', None, 'tp')
- w_out: bfloat16 [8, 16, 64, 1024], P('pp', 'tp')
- b_out: bfloat16 [8, 1024], P('pp')
- ln_par: bfloat16 [8, 4, 1024], P('pp')
- w_fc1: bfloat16 [8, 1024, 4096], P('pp', None, 'tp')
- b_fc1: bfloat16 [8, 4096], P('pp', 'tp')
- w_fc2: bfloat16 [8, 4096, 1024], P('pp', 'tp')
- b_fc2: bfloat16 [8, 1024], P('pp')
Outputs:
- output 1: bfloat16 [8, 2, 2, 384, 1024], P('pp', None, 'dp')
- output 2: bfloat16 [8, 2, 2, 384, 1024], P('pp', None, 'dp')
- output 3: float32 [8, 3, 1024, 16, 64], P(('dp', 'pp'), None, None, 'tp')
- output 4: float32 [8, 3, 16, 64], P(('dp', 'pp'), None, 'tp')
- output 5: float32 [8, 16, 64, 1024], P(('dp', 'pp'), 'tp')
- output 6: float32 [8, 1024], P(('dp', 'pp'))
- output 7: float32 [8, 4, 1024], P(('dp', 'pp'))
- output 8: float32 [8, 1024, 4096], P(('dp', 'pp'), None, 'tp')
- output 9: float32 [8, 4096], P(('dp', 'pp'), 'tp')
- output 10: float32 [8, 4096, 1024], P(('dp', 'pp'), 'tp')
- output 11: float32 [8, 1024], P(('dp', 'pp'))
All inputs are finite; a program needn't handle non-finite values.
Results may differ from a plain program's by a relative error of at most 0.02.
Values are sent between devices in bfloat16 or wider.
A program may use at most 768 MiB of HBM per device.

v0:
```python
import jax
import jax.numpy as jnp
from jax import lax
from jax.sharding import PartitionSpec as P

LN_EPS = 1e-5


def layer_norm(x_act, ln_gain, ln_shift):
    x_wide = x_act.astype(jnp.float32)
    row_mean = jnp.mean(x_wide, axis=-1, keepdims=True)
    centered = x_wide - row_mean
    row_var = jnp.mean(centered * centered, axis=-1, keepdims=True)
    normed = centered * lax.rsqrt(row_var + LN_EPS)
    return (normed * ln_gain + ln_shift).astype(jnp.bfloat16)


def causal_attention(q_heads, k_heads, v_heads):
    head_dim = q_heads.shape[-1]
    seq_len = q_heads.shape[1]
    scores = jnp.einsum("bqhe,bkhe->bhqk", q_heads, k_heads, preferred_element_type=jnp.float32) * (head_dim ** -0.5)
    row_pos = lax.broadcasted_iota(jnp.int32, (seq_len, seq_len), 0)
    col_pos = lax.broadcasted_iota(jnp.int32, (seq_len, seq_len), 1)
    scores = jnp.where(row_pos >= col_pos, scores, -1e30)
    attn_probs = jax.nn.softmax(scores, axis=-1).astype(jnp.bfloat16)
    attn_mix = jnp.einsum("bhqk,bkhe->bqhe", attn_probs, v_heads, preferred_element_type=jnp.float32)
    return attn_mix.astype(jnp.bfloat16)


def gelu_tanh(pre_act):
    return jax.nn.gelu(pre_act, approximate=True)


def layer_forward(x_act, layer_w):
    w_qkv, b_qkv, w_out, b_out, ln_par, w_fc1, b_fc1, w_fc2, b_fc2 = layer_w
    ln_wide = ln_par.astype(jnp.float32)
    h_one = layer_norm(x_act, ln_wide[0], ln_wide[1])
    qkv_all = (jnp.einsum("bsd,cdhe->bsche", h_one, w_qkv, preferred_element_type=jnp.float32) + b_qkv.astype(jnp.float32)).astype(jnp.bfloat16)
    attn_mix = causal_attention(qkv_all[:, :, 0], qkv_all[:, :, 1], qkv_all[:, :, 2])
    attn_part = jnp.einsum("bshe,hed->bsd", attn_mix, w_out, preferred_element_type=jnp.float32).astype(jnp.bfloat16)
    attn_sum = lax.psum(attn_part, "tp")
    x_mid = (x_act.astype(jnp.float32) + attn_sum.astype(jnp.float32) + b_out.astype(jnp.float32)).astype(jnp.bfloat16)
    h_two = layer_norm(x_mid, ln_wide[2], ln_wide[3])
    pre_act = jnp.einsum("bsd,df->bsf", h_two, w_fc1, preferred_element_type=jnp.float32) + b_fc1.astype(jnp.float32)
    gelu_out = gelu_tanh(pre_act).astype(jnp.bfloat16)
    mlp_part = jnp.einsum("bsf,fd->bsd", gelu_out, w_fc2, preferred_element_type=jnp.float32).astype(jnp.bfloat16)
    mlp_sum = lax.psum(mlp_part, "tp")
    y_act = (x_mid.astype(jnp.float32) + mlp_sum.astype(jnp.float32) + b_fc2.astype(jnp.float32)).astype(jnp.bfloat16)
    return y_act, qkv_all, x_mid, pre_act


def layer_backward(grad_out, x_act, qkv_all, x_mid, pre_act, layer_w):
    w_qkv = layer_w[0]
    w_out = layer_w[2]
    ln_wide = layer_w[4].astype(jnp.float32)
    w_fc1 = layer_w[5]
    w_fc2 = layer_w[7]
    grad_wide = grad_out.astype(jnp.float32)
    g_b_fc2 = jnp.sum(grad_wide, axis=(0, 1))
    gelu_wide, gelu_pull = jax.vjp(gelu_tanh, pre_act)
    gelu_out = gelu_wide.astype(jnp.bfloat16)
    g_w_fc2 = jnp.einsum("bsf,bsd->fd", gelu_out, grad_out, preferred_element_type=jnp.float32)
    g_gelu = jnp.einsum("bsd,fd->bsf", grad_out, w_fc2, preferred_element_type=jnp.float32).astype(jnp.bfloat16)
    g_pre = gelu_pull(g_gelu.astype(jnp.float32))[0]
    g_b_fc1 = jnp.sum(g_pre, axis=(0, 1))
    g_pre_half = g_pre.astype(jnp.bfloat16)
    h_two, ln_two_pull = jax.vjp(layer_norm, x_mid, ln_wide[2], ln_wide[3])
    g_w_fc1 = jnp.einsum("bsd,bsf->df", h_two, g_pre_half, preferred_element_type=jnp.float32)
    g_h_two = lax.psum(jnp.einsum("bsf,df->bsd", g_pre_half, w_fc1, preferred_element_type=jnp.float32).astype(jnp.bfloat16), "tp")
    g_mid_ln, g_gain_two, g_shift_two = ln_two_pull(g_h_two)
    g_mid_wide = grad_wide + g_mid_ln.astype(jnp.float32)
    g_mid = g_mid_wide.astype(jnp.bfloat16)
    g_b_out = jnp.sum(g_mid_wide, axis=(0, 1))
    attn_mix, attn_pull = jax.vjp(causal_attention, qkv_all[:, :, 0], qkv_all[:, :, 1], qkv_all[:, :, 2])
    g_w_out = jnp.einsum("bshe,bsd->hed", attn_mix, g_mid, preferred_element_type=jnp.float32)
    g_mix = jnp.einsum("bsd,hed->bshe", g_mid, w_out, preferred_element_type=jnp.float32).astype(jnp.bfloat16)
    g_query, g_key, g_value = attn_pull(g_mix)
    g_qkv = jnp.stack([g_query, g_key, g_value], axis=2)
    g_b_qkv = jnp.sum(g_qkv.astype(jnp.float32), axis=(0, 1))
    h_one, ln_one_pull = jax.vjp(layer_norm, x_act, ln_wide[0], ln_wide[1])
    g_w_qkv = jnp.einsum("bsd,bsche->cdhe", h_one, g_qkv, preferred_element_type=jnp.float32)
    g_h_one = lax.psum(jnp.einsum("bsche,cdhe->bsd", g_qkv, w_qkv, preferred_element_type=jnp.float32).astype(jnp.bfloat16), "tp")
    g_in_ln, g_gain_one, g_shift_one = ln_one_pull(g_h_one)
    grad_in = (g_mid_wide + g_in_ln.astype(jnp.float32)).astype(jnp.bfloat16)
    g_ln = jnp.stack([g_gain_one, g_shift_one, g_gain_two, g_shift_two])
    return grad_in, (g_w_qkv, g_b_qkv, g_w_out, g_b_out, g_ln, g_w_fc1, g_b_fc1, g_w_fc2, g_b_fc2)


def solution(mesh):
    stages = mesh.shape["pp"]
    tp_size = mesh.shape["tp"]
    fwd_pairs = [(src_idx, src_idx + 1) for src_idx in range(stages - 1)]
    back_pairs = [(src_idx + 1, src_idx) for src_idx in range(stages - 1)]

    def pass_on(boundary, stage_pairs):
        seq_part = boundary.shape[1] // tp_size
        own_part = lax.dynamic_slice_in_dim(boundary, lax.axis_index("tp") * seq_part, seq_part, axis=1)
        moved_part = lax.ppermute(own_part, "pp", stage_pairs)
        return lax.all_gather(moved_part, "tp", axis=1, tiled=True)

    def stage_program(x_in, dy_out, w_qkv, b_qkv, w_out, b_out, ln_par, w_fc1, b_fc1, w_fc2, b_fc2):
        layer_w = (w_qkv[0], b_qkv[0], w_out[0], b_out[0], ln_par[0], w_fc1[0], b_fc1[0], w_fc2[0], b_fc2[0])
        micro_count, batch_rows, seq_len, d_model = x_in.shape
        local_heads = w_qkv.shape[3]
        head_dim = w_qkv.shape[4]
        ff_local = w_fc1.shape[2]
        stage_idx = lax.axis_index("pp")
        last_stage = stages - 1
        step_count = micro_count + stages - 1
        act_shape = (batch_rows, seq_len, d_model)
        buf_len = micro_count + 1

        def fwd_step(fwd_carry, step_idx):
            received, x_buf, qkv_buf, mid_buf, pre_buf, out_buf = fwd_carry
            micro_idx = step_idx - stage_idx
            is_valid = (micro_idx >= 0) & (micro_idx < micro_count)
            read_idx = jnp.clip(micro_idx, 0, micro_count - 1)
            write_idx = jnp.where(is_valid, micro_idx, micro_count)
            x_first = lax.dynamic_index_in_dim(x_in, read_idx, 0, keepdims=False)
            x_act = jnp.where(stage_idx == 0, x_first, received)
            y_act, qkv_all, x_mid, pre_act = layer_forward(x_act, layer_w)
            x_buf = lax.dynamic_update_index_in_dim(x_buf, x_act, write_idx, 0)
            qkv_buf = lax.dynamic_update_index_in_dim(qkv_buf, qkv_all, write_idx, 0)
            mid_buf = lax.dynamic_update_index_in_dim(mid_buf, x_mid, write_idx, 0)
            pre_buf = lax.dynamic_update_index_in_dim(pre_buf, pre_act, write_idx, 0)
            out_buf = lax.dynamic_update_index_in_dim(out_buf, y_act, write_idx, 0)
            received = pass_on(y_act, fwd_pairs)
            return (received, x_buf, qkv_buf, mid_buf, pre_buf, out_buf), None

        fwd_init = (jnp.zeros(act_shape, jnp.bfloat16),
                    jnp.zeros((buf_len,) + act_shape, jnp.bfloat16),
                    jnp.zeros((buf_len, batch_rows, seq_len, 3, local_heads, head_dim), jnp.bfloat16),
                    jnp.zeros((buf_len,) + act_shape, jnp.bfloat16),
                    jnp.zeros((buf_len, batch_rows, seq_len, ff_local), jnp.float32),
                    jnp.zeros((buf_len,) + act_shape, jnp.bfloat16))
        fwd_final, _ = lax.scan(fwd_step, fwd_init, jnp.arange(step_count))
        _, x_buf, qkv_buf, mid_buf, pre_buf, out_buf = fwd_final

        def bwd_step(bwd_carry, step_idx):
            received, grad_acc, grad_buf = bwd_carry
            micro_idx = micro_count + last_stage - 1 - stage_idx - step_idx
            is_valid = (micro_idx >= 0) & (micro_idx < micro_count)
            read_idx = jnp.clip(micro_idx, 0, micro_count - 1)
            write_idx = jnp.where(is_valid, micro_idx, micro_count)
            dy_last = lax.dynamic_index_in_dim(dy_out, read_idx, 0, keepdims=False)
            grad_out = jnp.where(stage_idx == last_stage, dy_last, received)
            grad_out = jnp.where(is_valid, grad_out, jnp.zeros_like(grad_out))
            x_act = lax.dynamic_index_in_dim(x_buf, read_idx, 0, keepdims=False)
            qkv_all = lax.dynamic_index_in_dim(qkv_buf, read_idx, 0, keepdims=False)
            x_mid = lax.dynamic_index_in_dim(mid_buf, read_idx, 0, keepdims=False)
            pre_act = lax.dynamic_index_in_dim(pre_buf, read_idx, 0, keepdims=False)
            grad_in, layer_grads = layer_backward(grad_out, x_act, qkv_all, x_mid, pre_act, layer_w)
            grad_acc = tuple(acc_item + new_item for acc_item, new_item in zip(grad_acc, layer_grads))
            grad_buf = lax.dynamic_update_index_in_dim(grad_buf, grad_in, write_idx, 0)
            received = pass_on(grad_in, back_pairs)
            return (received, grad_acc, grad_buf), None

        grad_init = tuple(jnp.zeros(w_item.shape, jnp.float32) for w_item in layer_w)
        bwd_init = (jnp.zeros(act_shape, jnp.bfloat16), grad_init, jnp.zeros((buf_len,) + act_shape, jnp.bfloat16))
        bwd_final, _ = lax.scan(bwd_step, bwd_init, jnp.arange(step_count))
        _, grad_sum, grad_buf = bwd_final
        return (out_buf[:micro_count][None], grad_buf[:micro_count][None]) + tuple(g_item[None] for g_item in grad_sum)

    act_spec = P(None, "dp", None, None)
    arg_specs = (act_spec, act_spec,
                 P("pp", None, None, "tp", None), P("pp", None, "tp", None), P("pp", "tp", None, None),
                 P("pp", None), P("pp", None, None), P("pp", None, "tp"), P("pp", "tp"),
                 P("pp", "tp", None), P("pp", None))
    stage_spec = P("pp", None, "dp", None, None)
    grad_axes = ("dp", "pp")
    result_specs = (stage_spec, stage_spec,
                    P(grad_axes, None, None, "tp", None), P(grad_axes, None, "tp", None), P(grad_axes, "tp", None, None),
                    P(grad_axes, None), P(grad_axes, None, None), P(grad_axes, None, "tp"), P(grad_axes, "tp"),
                    P(grad_axes, "tp", None), P(grad_axes, None))
    return jax.shard_map(stage_program, mesh=mesh, in_specs=arg_specs, out_specs=result_specs, check_vma=False)
```

profile of v0, /device:TPU:97, one launch (start us, length us, event | category | flops | bytes accessed | tf_op | source)
XLA Modules:
  0.0 3021.0 jit_solution(10856181210972478463)
XLA Ops:
  26.2 1426.9 %while.54 = (s32[]{:T(128)}, bf16[2,384,1024]{2,1,0:T(8,128)(2,1)}, bf16[3,2,384,1024]{3,2,1,0:T(8,128)(2,1)}, bf16[3,2,384,3,4,64]{2,5,4,3,1,0:T(8,128)(2,1)}, ...) while((s32[]{:T(128)}, bf16[2,384,1024]{2,1,0:T(8,128)(2,1)}, ...), condition=%wide.region_9.10_spmd, body=%wide.region_0.9_spmd.sunk | while | flops 5181756928 | bytes 112403168 | solution.py:136
  44.5 49.3 %all-reduce.5.cloned.1.call-done = bf16[2,384,1024]{2,1,0:T(8,128)(2,1)} async-done(((bf16[2,384,1024]{2,1,0:T(8,128)(2,1)}), bf16[2,384,1024]{2,1,0:T(8,128)(2,1)}) %all-reduce.5.cloned.1.call-update) | async-done | bytes 1572880 | tf_op jit(solution)/shard_map/while/body/eval_jaxpr/psum | solution.py:41
  105.9 45.3 %all-reduce.7.cloned.1.call-done = bf16[2,384,1024]{2,1,0:T(8,128)(2,1)} async-done(((bf16[2,384,1024]{2,1,0:T(8,128)(2,1)}), bf16[2,384,1024]{2,1,0:T(8,128)(2,1)}) %all-reduce.7.cloned.1.call-update) | async-done | bytes 1572880 | tf_op jit(solution)/shard_map/while/body/eval_jaxpr/psum | solution.py:47
  163.8 24.3 all-gather.3.cloned.1.call-done
  206.2 45.7 %all-reduce.5.cloned.1.call-done = bf16[2,384,1024]{2,1,0:T(8,128)(2,1)} async-done(((bf16[2,384,1024]{2,1,0:T(8,128)(2,1)}), bf16[2,384,1024]{2,1,0:T(8,128)(2,1)}) %all-reduce.5.cloned.1.call-update) | async-done | bytes 1572880 | tf_op jit(solution)/shard_map/while/body/eval_jaxpr/psum | solution.py:41
  264.0 45.4 %all-reduce.7.cloned.1.call-done = bf16[2,384,1024]{2,1,0:T(8,128)(2,1)} async-done(((bf16[2,384,1024]{2,1,0:T(8,128)(2,1)}), bf16[2,384,1024]{2,1,0:T(8,128)(2,1)}) %all-reduce.7.cloned.1.call-update) | async-done | bytes 1572880 | tf_op jit(solution)/shard_map/while/body/eval_jaxpr/psum | solution.py:47
  322.0 24.3 all-gather.3.cloned.1.call-done
  364.3 45.8 %all-reduce.5.cloned.1.call-done = bf16[2,384,1024]{2,1,0:T(8,128)(2,1)} async-done(((bf16[2,384,1024]{2,1,0:T(8,128)(2,1)}), bf16[2,384,1024]{2,1,0:T(8,128)(2,1)}) %all-reduce.5.cloned.1.call-update) | async-done | bytes 1572880 | tf_op jit(solution)/shard_map/while/body/eval_jaxpr/psum | solution.py:41
  422.2 45.4 %all-reduce.7.cloned.1.call-done = bf16[2,384,1024]{2,1,0:T(8,128)(2,1)} async-done(((bf16[2,384,1024]{2,1,0:T(8,128)(2,1)}), bf16[2,384,1024]{2,1,0:T(8,128)(2,1)}) %all-reduce.7.cloned.1.call-update) | async-done | bytes 1572880 | tf_op jit(solution)/shard_map/while/body/eval_jaxpr/psum | solution.py:47
  480.1 24.4 all-gather.3.cloned.1.call-done
  522.5 45.8 %all-reduce.5.cloned.1.call-done = bf16[2,384,1024]{2,1,0:T(8,128)(2,1)} async-done(((bf16[2,384,1024]{2,1,0:T(8,128)(2,1)}), bf16[2,384,1024]{2,1,0:T(8,128)(2,1)}) %all-reduce.5.cloned.1.call-update) | async-done | bytes 1572880 | tf_op jit(solution)/shard_map/while/body/eval_jaxpr/psum | solution.py:41
  580.4 45.3 %all-reduce.7.cloned.1.call-done = bf16[2,384,1024]{2,1,0:T(8,128)(2,1)} async-done(((bf16[2,384,1024]{2,1,0:T(8,128)(2,1)}), bf16[2,384,1024]{2,1,0:T(8,128)(2,1)}) %all-reduce.7.cloned.1.call-update) | async-done | bytes 1572880 | tf_op jit(solution)/shard_map/while/body/eval_jaxpr/psum | solution.py:47
  638.2 24.4 all-gather.3.cloned.1.call-done
  680.6 45.8 %all-reduce.5.cloned.1.call-done = bf16[2,384,1024]{2,1,0:T(8,128)(2,1)} async-done(((bf16[2,384,1024]{2,1,0:T(8,128)(2,1)}), bf16[2,384,1024]{2,1,0:T(8,128)(2,1)}) %all-reduce.5.cloned.1.call-update) | async-done | bytes 1572880 | tf_op jit(solution)/shard_map/while/body/eval_jaxpr/psum | solution.py:41
  738.6 45.2 %all-reduce.7.cloned.1.call-done = bf16[2,384,1024]{2,1,0:T(8,128)(2,1)} async-done(((bf16[2,384,1024]{2,1,0:T(8,128)(2,1)}), bf16[2,384,1024]{2,1,0:T(8,128)(2,1)}) %all-reduce.7.cloned.1.call-update) | async-done | bytes 1572880 | tf_op jit(solution)/shard_map/while/body/eval_jaxpr/psum | solution.py:47
  796.3 24.3 all-gather.3.cloned.1.call-done
  838.7 45.7 %all-reduce.5.cloned.1.call-done = bf16[2,384,1024]{2,1,0:T(8,128)(2,1)} async-done(((bf16[2,384,1024]{2,1,0:T(8,128)(2,1)}), bf16[2,384,1024]{2,1,0:T(8,128)(2,1)}) %all-reduce.5.cloned.1.call-update) | async-done | bytes 1572880 | tf_op jit(solution)/shard_map/while/body/eval_jaxpr/psum | solution.py:41
  896.5 45.3 %all-reduce.7.cloned.1.call-done = bf16[2,384,1024]{2,1,0:T(8,128)(2,1)} async-done(((bf16[2,384,1024]{2,1,0:T(8,128)(2,1)}), bf16[2,384,1024]{2,1,0:T(8,128)(2,1)}) %all-reduce.7.cloned.1.call-update) | async-done | bytes 1572880 | tf_op jit(solution)/shard_map/while/body/eval_jaxpr/psum | solution.py:47
  954.3 24.3 all-gather.3.cloned.1.call-done
  996.7 45.8 %all-reduce.5.cloned.1.call-done = bf16[2,384,1024]{2,1,0:T(8,128)(2,1)} async-done(((bf16[2,384,1024]{2,1,0:T(8,128)(2,1)}), bf16[2,384,1024]{2,1,0:T(8,128)(2,1)}) %all-reduce.5.cloned.1.call-update) | async-done | bytes 1572880 | tf_op jit(solution)/shard_map/while/body/eval_jaxpr/psum | solution.py:41
  1054.6 45.3 %all-reduce.7.cloned.1.call-done = bf16[2,384,1024]{2,1,0:T(8,128)(2,1)} async-done(((bf16[2,384,1024]{2,1,0:T(8,128)(2,1)}), bf16[2,384,1024]{2,1,0:T(8,128)(2,1)}) %all-reduce.7.cloned.1.call-update) | async-done | bytes 1572880 | tf_op jit(solution)/shard_map/while/body/eval_jaxpr/psum | solution.py:47
  1112.4 24.3 all-gather.3.cloned.1.call-done
  1154.8 45.8 %all-reduce.5.cloned.1.call-done = bf16[2,384,1024]{2,1,0:T(8,128)(2,1)} async-done(((bf16[2,384,1024]{2,1,0:T(8,128)(2,1)}), bf16[2,384,1024]{2,1,0:T(8,128)(2,1)}) %all-reduce.5.cloned.1.call-update) | async-done | bytes 1572880 | tf_op jit(solution)/shard_map/while/body/eval_jaxpr/psum | solution.py:41
  1212.7 45.3 %all-reduce.7.cloned.1.call-done = bf16[2,384,1024]{2,1,0:T(8,128)(2,1)} async-done(((bf16[2,384,1024]{2,1,0:T(8,128)(2,1)}), bf16[2,384,1024]{2,1,0:T(8,128)(2,1)}) %all-reduce.7.cloned.1.call-update) | async-done | bytes 1572880 | tf_op jit(solution)/shard_map/while/body/eval_jaxpr/psum | solution.py:47
  1270.6 24.3 all-gather.3.cloned.1.call-done
  1313.0 45.8 %all-reduce.5.cloned.1.call-done = bf16[2,384,1024]{2,1,0:T(8,128)(2,1)} async-done(((bf16[2,384,1024]{2,1,0:T(8,128)(2,1)}), bf16[2,384,1024]{2,1,0:T(8,128)(2,1)}) %all-reduce.5.cloned.1.call-update) | async-done | bytes 1572880 | tf_op jit(solution)/shard_map/while/body/eval_jaxpr/psum | solution.py:41
  1370.9 45.3 %all-reduce.7.cloned.1.call-done = bf16[2,384,1024]{2,1,0:T(8,128)(2,1)} async-done(((bf16[2,384,1024]{2,1,0:T(8,128)(2,1)}), bf16[2,384,1024]{2,1,0:T(8,128)(2,1)}) %all-reduce.7.cloned.1.call-update) | async-done | bytes 1572880 | tf_op jit(solution)/shard_map/while/body/eval_jaxpr/psum | solution.py:47
  1428.7 24.3 all-gather.3.cloned.1.call-done
  1457.8 1549.9 %while.55 = (s32[]{:T(128)}, bf16[2,384,1024]{2,1,0:T(8,128)(2,1)}, f32[3,1024,4,64]{1,3,2,0:T(8,128)}, f32[3,4,64]{2,1,0:T(4,128)}, f32[4,64,1024]{2,1,0:T(8,12...) while((s32[]{:T(128)}, bf16[2,384,1024]{2,1,0:T(8,128)(2,1)}, ...), condition=%wide.region_32.33_spmd.clone, body=%wide.region_10.32_spmd.clone.sunk | while | flops 10715121664 | bytes 247793168 | solution.py:160
  1496.8 38.0 %all-reduce.9.cloned.1.call-done = bf16[2,384,1024]{2,1,0:T(8,128)(2,1)} async-done(((bf16[2,384,1024]{2,1,0:T(8,128)(2,1)}), bf16[2,384,1024]{2,1,0:T(8,128)(2,1)}) %all-reduce.9.cloned.1.call-update) | async-done | bytes 1572880 | tf_op jit(solution)/shard_map/while/body/eval_jaxpr/psum | solution.py:69
  1564.8 37.0 %all-reduce.11.cloned.1.call-done = bf16[2,384,1024]{2,1,0:T(8,128)(2,1)} async-done(((bf16[2,384,1024]{2,1,0:T(8,128)(2,1)}), bf16[2,384,1024]{2,1,0:T(8,128)(2,1)}) %all-reduce.11.cloned.1.call-update) | async-done | bytes 1572880 | tf_op jit(solution)/shard_map/while/body/eval_jaxpr/psum | solution.py:82
  1638.9 6.8 all-gather.5.cloned.1.call-done
  1667.1 38.0 %all-reduce.9.cloned.1.call-done = bf16[2,384,1024]{2,1,0:T(8,128)(2,1)} async-done(((bf16[2,384,1024]{2,1,0:T(8,128)(2,1)}), bf16[2,384,1024]{2,1,0:T(8,128)(2,1)}) %all-reduce.9.cloned.1.call-update) | async-done | bytes 1572880 | tf_op jit(solution)/shard_map/while/body/eval_jaxpr/psum | solution.py:69
  1729.0 7.3 bitcast_add_fusion.8
  1736.3 35.8 %all-reduce.11.cloned.1.call-done = bf16[2,384,1024]{2,1,0:T(8,128)(2,1)} async-done(((bf16[2,384,1024]{2,1,0:T(8,128)(2,1)}), bf16[2,384,1024]{2,1,0:T(8,128)(2,1)}) %all-reduce.11.cloned.1.call-update) | async-done | bytes 1572880 | tf_op jit(solution)/shard_map/while/body/eval_jaxpr/psum | solution.py:82
  1798.6 7.3 bitcast_add_fusion.7
  1837.3 38.0 %all-reduce.9.cloned.1.call-done = bf16[2,384,1024]{2,1,0:T(8,128)(2,1)} async-done(((bf16[2,384,1024]{2,1,0:T(8,128)(2,1)}), bf16[2,384,1024]{2,1,0:T(8,128)(2,1)}) %all-reduce.9.cloned.1.call-update) | async-done | bytes 1572880 | tf_op jit(solution)/shard_map/while/body/eval_jaxpr/psum | solution.py:69
  1899.2 7.3 bitcast_add_fusion.8
  1906.6 35.8 %all-reduce.11.cloned.1.call-done = bf16[2,384,1024]{2,1,0:T(8,128)(2,1)} async-done(((bf16[2,384,1024]{2,1,0:T(8,128)(2,1)}), bf16[2,384,1024]{2,1,0:T(8,128)(2,1)}) %all-reduce.11.cloned.1.call-update) | async-done | bytes 1572880 | tf_op jit(solution)/shard_map/while/body/eval_jaxpr/psum | solution.py:82
  1968.9 7.3 bitcast_add_fusion.7
  2007.6 38.0 %all-reduce.9.cloned.1.call-done = bf16[2,384,1024]{2,1,0:T(8,128)(2,1)} async-done(((bf16[2,384,1024]{2,1,0:T(8,128)(2,1)}), bf16[2,384,1024]{2,1,0:T(8,128)(2,1)}) %all-reduce.9.cloned.1.call-update) | async-done | bytes 1572880 | tf_op jit(solution)/shard_map/while/body/eval_jaxpr/psum | solution.py:69
  2069.5 7.3 bitcast_add_fusion.8
  2076.8 35.8 %all-reduce.11.cloned.1.call-done = bf16[2,384,1024]{2,1,0:T(8,128)(2,1)} async-done(((bf16[2,384,1024]{2,1,0:T(8,128)(2,1)}), bf16[2,384,1024]{2,1,0:T(8,128)(2,1)}) %all-reduce.11.cloned.1.call-update) | async-done | bytes 1572880 | tf_op jit(solution)/shard_map/while/body/eval_jaxpr/psum | solution.py:82
  2139.1 7.3 bitcast_add_fusion.7
  2177.8 38.0 %all-reduce.9.cloned.1.call-done = bf16[2,384,1024]{2,1,0:T(8,128)(2,1)} async-done(((bf16[2,384,1024]{2,1,0:T(8,128)(2,1)}), bf16[2,384,1024]{2,1,0:T(8,128)(2,1)}) %all-reduce.9.cloned.1.call-update) | async-done | bytes 1572880 | tf_op jit(solution)/shard_map/while/body/eval_jaxpr/psum | solution.py:69
  2239.7 7.3 bitcast_add_fusion.8
  2247.0 35.8 %all-reduce.11.cloned.1.call-done = bf16[2,384,1024]{2,1,0:T(8,128)(2,1)} async-done(((bf16[2,384,1024]{2,1,0:T(8,128)(2,1)}), bf16[2,384,1024]{2,1,0:T(8,128)(2,1)}) %all-reduce.11.cloned.1.call-update) | async-done | bytes 1572880 | tf_op jit(solution)/shard_map/while/body/eval_jaxpr/psum | solution.py:82
  2309.3 7.3 bitcast_add_fusion.7
  2348.1 38.0 %all-reduce.9.cloned.1.call-done = bf16[2,384,1024]{2,1,0:T(8,128)(2,1)} async-done(((bf16[2,384,1024]{2,1,0:T(8,128)(2,1)}), bf16[2,384,1024]{2,1,0:T(8,128)(2,1)}) %all-reduce.9.cloned.1.call-update) | async-done | bytes 1572880 | tf_op jit(solution)/shard_map/while/body/eval_jaxpr/psum | solution.py:69
  2409.9 7.3 bitcast_add_fusion.8
  2417.3 35.8 %all-reduce.11.cloned.1.call-done = bf16[2,384,1024]{2,1,0:T(8,128)(2,1)} async-done(((bf16[2,384,1024]{2,1,0:T(8,128)(2,1)}), bf16[2,384,1024]{2,1,0:T(8,128)(2,1)}) %all-reduce.11.cloned.1.call-update) | async-done | bytes 1572880 | tf_op jit(solution)/shard_map/while/body/eval_jaxpr/psum | solution.py:82
  2479.6 7.3 bitcast_add_fusion.7
  2518.3 38.0 %all-reduce.9.cloned.1.call-done = bf16[2,384,1024]{2,1,0:T(8,128)(2,1)} async-done(((bf16[2,384,1024]{2,1,0:T(8,128)(2,1)}), bf16[2,384,1024]{2,1,0:T(8,128)(2,1)}) %all-reduce.9.cloned.1.call-update) | async-done | bytes 1572880 | tf_op jit(solution)/shard_map/while/body/eval_jaxpr/psum | solution.py:69
  2580.2 7.3 bitcast_add_fusion.8
  2587.5 35.8 %all-reduce.11.cloned.1.call-done = bf16[2,384,1024]{2,1,0:T(8,128)(2,1)} async-done(((bf16[2,384,1024]{2,1,0:T(8,128)(2,1)}), bf16[2,384,1024]{2,1,0:T(8,128)(2,1)}) %all-reduce.11.cloned.1.call-update) | async-done | bytes 1572880 | tf_op jit(solution)/shard_map/while/body/eval_jaxpr/psum | solution.py:82
  2649.8 7.3 bitcast_add_fusion.7
  2688.5 38.0 %all-reduce.9.cloned.1.call-done = bf16[2,384,1024]{2,1,0:T(8,128)(2,1)} async-done(((bf16[2,384,1024]{2,1,0:T(8,128)(2,1)}), bf16[2,384,1024]{2,1,0:T(8,128)(2,1)}) %all-reduce.9.cloned.1.call-update) | async-done | bytes 1572880 | tf_op jit(solution)/shard_map/while/body/eval_jaxpr/psum | solution.py:69
  2750.4 7.3 bitcast_add_fusion.8
  2757.8 35.8 %all-reduce.11.cloned.1.call-done = bf16[2,384,1024]{2,1,0:T(8,128)(2,1)} async-done(((bf16[2,384,1024]{2,1,0:T(8,128)(2,1)}), bf16[2,384,1024]{2,1,0:T(8,128)(2,1)}) %all-reduce.11.cloned.1.call-update) | async-done | bytes 1572880 | tf_op jit(solution)/shard_map/while/body/eval_jaxpr/psum | solution.py:82
  2820.1 7.3 bitcast_add_fusion.7
  2858.8 38.0 %all-reduce.9.cloned.1.call-done = bf16[2,384,1024]{2,1,0:T(8,128)(2,1)} async-done(((bf16[2,384,1024]{2,1,0:T(8,128)(2,1)}), bf16[2,384,1024]{2,1,0:T(8,128)(2,1)}) %all-reduce.9.cloned.1.call-update) | async-done | bytes 1572880 | tf_op jit(solution)/shard_map/while/body/eval_jaxpr/psum | solution.py:69
  2920.7 7.3 bitcast_add_fusion.8
  2928.0 35.8 %all-reduce.11.cloned.1.call-done = bf16[2,384,1024]{2,1,0:T(8,128)(2,1)} async-done(((bf16[2,384,1024]{2,1,0:T(8,128)(2,1)}), bf16[2,384,1024]{2,1,0:T(8,128)(2,1)}) %all-reduce.11.cloned.1.call-update) | async-done | bytes 1572880 | tf_op jit(solution)/shard_map/while/body/eval_jaxpr/psum | solution.py:82
  2990.3 7.3 bitcast_add_fusion.7
  (1342 shorter events, 1140.9 us)
Async XLA Ops:
  26.4 67.5 %all-reduce.5.cloned.1.call-start = ((), (), s32[]{:S(2)}) async-start(), calls=%async_computation | async-start | bytes 3145728 | tf_op jit(solution)/shard_map/while/body/eval_jaxpr/psum | solution.py:41
  44.4 106.9 %all-reduce.7.cloned.1.call-start = ((), (), s32[]{:S(2)}) async-start(), calls=%async_computation.1 | async-start | bytes 3145728 | tf_op jit(solution)/shard_map/while/body/eval_jaxpr/psum | solution.py:47
  105.9 82.3 %all-gather.3.cloned.1.call-start = ((), (), s32[]{:S(2)}) async-start(), calls=%async_computation.2 | async-start | bytes 1966080 | tf_op jit(solution)/shard_map/while/body/eval_jaxpr/all_gather | solution.py:99
  188.2 63.8 %all-reduce.5.cloned.1.call-start = ((), (), s32[]{:S(2)}) async-start(), calls=%async_computation | async-start | bytes 3145728 | tf_op jit(solution)/shard_map/while/body/eval_jaxpr/psum | solution.py:41
  206.1 103.3 %all-reduce.7.cloned.1.call-start = ((), (), s32[]{:S(2)}) async-start(), calls=%async_computation.1 | async-start | bytes 3145728 | tf_op jit(solution)/shard_map/while/body/eval_jaxpr/psum | solution.py:47
  263.9 82.4 %all-gather.3.cloned.1.call-start = ((), (), s32[]{:S(2)}) async-start(), calls=%async_computation.2 | async-start | bytes 1966080 | tf_op jit(solution)/shard_map/while/body/eval_jaxpr/all_gather | solution.py:99
  312.7 8.4 collective-permute-start
  346.3 63.8 %all-reduce.5.cloned.1.call-start = ((), (), s32[]{:S(2)}) async-start(), calls=%async_computation | async-start | bytes 3145728 | tf_op jit(solution)/shard_map/while/body/eval_jaxpr/psum | solution.py:41
  364.2 103.4 %all-reduce.7.cloned.1.call-start = ((), (), s32[]{:S(2)}) async-start(), calls=%async_computation.1 | async-start | bytes 3145728 | tf_op jit(solution)/shard_map/while/body/eval_jaxpr/psum | solution.py:47
  422.1 82.4 %all-gather.3.cloned.1.call-start = ((), (), s32[]{:S(2)}) async-start(), calls=%async_computation.2 | async-start | bytes 1966080 | tf_op jit(solution)/shard_map/while/body/eval_jaxpr/all_gather | solution.py:99
  504.5 63.8 %all-reduce.5.cloned.1.call-start = ((), (), s32[]{:S(2)}) async-start(), calls=%async_computation | async-start | bytes 3145728 | tf_op jit(solution)/shard_map/while/body/eval_jaxpr/psum | solution.py:41
  522.4 103.3 %all-reduce.7.cloned.1.call-start = ((), (), s32[]{:S(2)}) async-start(), calls=%async_computation.1 | async-start | bytes 3145728 | tf_op jit(solution)/shard_map/while/body/eval_jaxpr/psum | solution.py:47
  580.3 82.3 %all-gather.3.cloned.1.call-start = ((), (), s32[]{:S(2)}) async-start(), calls=%async_computation.2 | async-start | bytes 1966080 | tf_op jit(solution)/shard_map/while/body/eval_jaxpr/all_gather | solution.py:99
  662.6 63.8 %all-reduce.5.cloned.1.call-start = ((), (), s32[]{:S(2)}) async-start(), calls=%async_computation | async-start | bytes 3145728 | tf_op jit(solution)/shard_map/while/body/eval_jaxpr/psum | solution.py:41
  680.6 103.2 %all-reduce.7.cloned.1.call-start = ((), (), s32[]{:S(2)}) async-start(), calls=%async_computation.1 | async-start | bytes 3145728 | tf_op jit(solution)/shard_map/while/body/eval_jaxpr/psum | solution.py:47
  738.5 82.2 %all-gather.3.cloned.1.call-start = ((), (), s32[]{:S(2)}) async-start(), calls=%async_computation.2 | async-start | bytes 1966080 | tf_op jit(solution)/shard_map/while/body/eval_jaxpr/all_gather | solution.py:99
  820.6 63.8 %all-reduce.5.cloned.1.call-start = ((), (), s32[]{:S(2)}) async-start(), calls=%async_computation | async-start | bytes 3145728 | tf_op jit(solution)/shard_map/while/body/eval_jaxpr/psum | solution.py:41
  838.6 103.2 %all-reduce.7.cloned.1.call-start = ((), (), s32[]{:S(2)}) async-start(), calls=%async_computation.1 | async-start | bytes 3145728 | tf_op jit(solution)/shard_map/while/body/eval_jaxpr/psum | solution.py:47
  896.4 82.2 %all-gather.3.cloned.1.call-start = ((), (), s32[]{:S(2)}) async-start(), calls=%async_computation.2 | async-start | bytes 1966080 | tf_op jit(solution)/shard_map/while/body/eval_jaxpr/all_gather | solution.py:99
  978.6 63.8 %all-reduce.5.cloned.1.call-start = ((), (), s32[]{:S(2)}) async-start(), calls=%async_computation | async-start | bytes 3145728 | tf_op jit(solution)/shard_map/while/body/eval_jaxpr/psum | solution.py:41
  996.6 103.3 %all-reduce.7.cloned.1.call-start = ((), (), s32[]{:S(2)}) async-start(), calls=%async_computation.1 | async-start | bytes 3145728 | tf_op jit(solution)/shard_map/while/body/eval_jaxpr/psum | solution.py:47
  1054.5 82.3 %all-gather.3.cloned.1.call-start = ((), (), s32[]{:S(2)}) async-start(), calls=%async_computation.2 | async-start | bytes 1966080 | tf_op jit(solution)/shard_map/while/body/eval_jaxpr/all_gather | solution.py:99
  1136.8 63.8 %all-reduce.5.cloned.1.call-start = ((), (), s32[]{:S(2)}) async-start(), calls=%async_computation | async-start | bytes 3145728 | tf_op jit(solution)/shard_map/while/body/eval_jaxpr/psum | solution.py:41
  1154.7 103.3 %all-reduce.7.cloned.1.call-start = ((), (), s32[]{:S(2)}) async-start(), calls=%async_computation.1 | async-start | bytes 3145728 | tf_op jit(solution)/shard_map/while/body/eval_jaxpr/psum | solution.py:47
  1212.6 82.3 %all-gather.3.cloned.1.call-start = ((), (), s32[]{:S(2)}) async-start(), calls=%async_computation.2 | async-start | bytes 1966080 | tf_op jit(solution)/shard_map/while/body/eval_jaxpr/all_gather | solution.py:99
  1294.9 63.8 %all-reduce.5.cloned.1.call-start = ((), (), s32[]{:S(2)}) async-start(), calls=%async_computation | async-start | bytes 3145728 | tf_op jit(solution)/shard_map/while/body/eval_jaxpr/psum | solution.py:41
  1312.9 103.3 %all-reduce.7.cloned.1.call-start = ((), (), s32[]{:S(2)}) async-start(), calls=%async_computation.1 | async-start | bytes 3145728 | tf_op jit(solution)/shard_map/while/body/eval_jaxpr/psum | solution.py:47
  1370.8 82.3 %all-gather.3.cloned.1.call-start = ((), (), s32[]{:S(2)}) async-start(), calls=%async_computation.2 | async-start | bytes 1966080 | tf_op jit(solution)/shard_map/while/body/eval_jaxpr/all_gather | solution.py:99
  1475.4 59.4 %all-reduce.9.cloned.1.call-start = ((), (), s32[]{:S(2)}) async-start(), calls=%async_computation.3 | async-start | bytes 3145728 | tf_op jit(solution)/shard_map/while/body/eval_jaxpr/psum | solution.py:69
  1488.9 112.9 %all-reduce.11.cloned.1.call-start = ((), (), s32[]{:S(2)}) async-start(), calls=%async_computation.4 | async-start | bytes 3145728 | tf_op jit(solution)/shard_map/while/body/eval_jaxpr/psum | solution.py:82
  1556.4 89.3 %all-gather.5.cloned.1.call-start = ((), (), s32[]{:S(2)}) async-start(), calls=%async_computation.5 | async-start | bytes 1966080 | tf_op jit(solution)/shard_map/while/body/eval_jaxpr/all_gather | solution.py:99
  1613.8 9.1 collective-permute-start.1
  1645.7 59.3 %all-reduce.9.cloned.1.call-start = ((), (), s32[]{:S(2)}) async-start(), calls=%async_computation.3 | async-start | bytes 3145728 | tf_op jit(solution)/shard_map/while/body/eval_jaxpr/psum | solution.py:69
  1659.2 112.9 %all-reduce.11.cloned.1.call-start = ((), (), s32[]{:S(2)}) async-start(), calls=%async_computation.4 | async-start | bytes 3145728 | tf_op jit(solution)/shard_map/while/body/eval_jaxpr/psum | solution.py:82
  1726.6 89.3 %all-gather.5.cloned.1.call-start = ((), (), s32[]{:S(2)}) async-start(), calls=%async_computation.5 | async-start | bytes 1966080 | tf_op jit(solution)/shard_map/while/body/eval_jaxpr/all_gather | solution.py:99
  1784.0 9.1 collective-permute-start.1
  1816.0 59.3 %all-reduce.9.cloned.1.call-start = ((), (), s32[]{:S(2)}) async-start(), calls=%async_computation.3 | async-start | bytes 3145728 | tf_op jit(solution)/shard_map/while/body/eval_jaxpr/psum | solution.py:69
  1829.4 112.9 %all-reduce.11.cloned.1.call-start = ((), (), s32[]{:S(2)}) async-start(), calls=%async_computation.4 | async-start | bytes 3145728 | tf_op jit(solution)/shard_map/while/body/eval_jaxpr/psum | solution.py:82
  1896.9 89.4 %all-gather.5.cloned.1.call-start = ((), (), s32[]{:S(2)}) async-start(), calls=%async_computation.5 | async-start | bytes 1966080 | tf_op jit(solution)/shard_map/while/body/eval_jaxpr/all_gather | solution.py:99
  1954.3 9.1 collective-permute-start.1
  1986.2 59.3 %all-reduce.9.cloned.1.call-start = ((), (), s32[]{:S(2)}) async-start(), calls=%async_computation.3 | async-start | bytes 3145728 | tf_op jit(solution)/shard_map/while/body/eval_jaxpr/psum | solution.py:69
  1999.7 112.9 %all-reduce.11.cloned.1.call-start = ((), (), s32[]{:S(2)}) async-start(), calls=%async_computation.4 | async-start | bytes 3145728 | tf_op jit(solution)/shard_map/while/body/eval_jaxpr/psum | solution.py:82
  2067.1 89.3 %all-gather.5.cloned.1.call-start = ((), (), s32[]{:S(2)}) async-start(), calls=%async_computation.5 | async-start | bytes 1966080 | tf_op jit(solution)/shard_map/while/body/eval_jaxpr/all_gather | solution.py:99
  2124.5 9.1 collective-permute-start.1
  2156.5 59.3 %all-reduce.9.cloned.1.call-start = ((), (), s32[]{:S(2)}) async-start(), calls=%async_computation.3 | async-start | bytes 3145728 | tf_op jit(solution)/shard_map/while/body/eval_jaxpr/psum | solution.py:69
  2169.9 112.9 %all-reduce.11.cloned.1.call-start = ((), (), s32[]{:S(2)}) async-start(), calls=%async_computation.4 | async-start | bytes 3145728 | tf_op jit(solution)/shard_map/while/body/eval_jaxpr/psum | solution.py:82
  2237.4 89.3 %all-gather.5.cloned.1.call-start = ((), (), s32[]{:S(2)}) async-start(), calls=%async_computation.5 | async-start | bytes 1966080 | tf_op jit(solution)/shard_map/while/body/eval_jaxpr/all_gather | solution.py:99
  2294.8 9.1 collective-permute-start.1
  2326.7 59.3 %all-reduce.9.cloned.1.call-start = ((), (), s32[]{:S(2)}) async-start(), calls=%async_computation.3 | async-start | bytes 3145728 | tf_op jit(solution)/shard_map/while/body/eval_jaxpr/psum | solution.py:69
  2340.2 112.9 %all-reduce.11.cloned.1.call-start = ((), (), s32[]{:S(2)}) async-start(), calls=%async_computation.4 | async-start | bytes 3145728 | tf_op jit(solution)/shard_map/while/body/eval_jaxpr/psum | solution.py:82
  2407.6 89.3 %all-gather.5.cloned.1.call-start = ((), (), s32[]{:S(2)}) async-start(), calls=%async_computation.5 | async-start | bytes 1966080 | tf_op jit(solution)/shard_map/while/body/eval_jaxpr/all_gather | solution.py:99
  2465.0 9.1 collective-permute-start.1
  2497.0 59.3 %all-reduce.9.cloned.1.call-start = ((), (), s32[]{:S(2)}) async-start(), calls=%async_computation.3 | async-start | bytes 3145728 | tf_op jit(solution)/shard_map/while/body/eval_jaxpr/psum | solution.py:69
  2510.4 112.9 %all-reduce.11.cloned.1.call-start = ((), (), s32[]{:S(2)}) async-start(), calls=%async_computation.4 | async-start | bytes 3145728 | tf_op jit(solution)/shard_map/while/body/eval_jaxpr/psum | solution.py:82
  2577.9 89.3 %all-gather.5.cloned.1.call-start = ((), (), s32[]{:S(2)}) async-start(), calls=%async_computation.5 | async-start | bytes 1966080 | tf_op jit(solution)/shard_map/while/body/eval_jaxpr/all_gather | solution.py:99
  2635.2 9.1 collective-permute-start.1
  2667.2 59.3 %all-reduce.9.cloned.1.call-start = ((), (), s32[]{:S(2)}) async-start(), calls=%async_computation.3 | async-start | bytes 3145728 | tf_op jit(solution)/shard_map/while/body/eval_jaxpr/psum | solution.py:69
  2680.7 112.9 %all-reduce.11.cloned.1.call-start = ((), (), s32[]{:S(2)}) async-start(), calls=%async_computation.4 | async-start | bytes 3145728 | tf_op jit(solution)/shard_map/while/body/eval_jaxpr/psum | solution.py:82
  2748.1 89.3 %all-gather.5.cloned.1.call-start = ((), (), s32[]{:S(2)}) async-start(), calls=%async_computation.5 | async-start | bytes 1966080 | tf_op jit(solution)/shard_map/while/body/eval_jaxpr/all_gather | solution.py:99
  2805.5 9.1 collective-permute-start.1
  2837.4 59.3 %all-reduce.9.cloned.1.call-start = ((), (), s32[]{:S(2)}) async-start(), calls=%async_computation.3 | async-start | bytes 3145728 | tf_op jit(solution)/shard_map/while/body/eval_jaxpr/psum | solution.py:69
  2850.9 112.9 %all-reduce.11.cloned.1.call-start = ((), (), s32[]{:S(2)}) async-start(), calls=%async_computation.4 | async-start | bytes 3145728 | tf_op jit(solution)/shard_map/while/body/eval_jaxpr/psum | solution.py:82
  2918.3 89.3 %all-gather.5.cloned.1.call-start = ((), (), s32[]{:S(2)}) async-start(), calls=%async_computation.5 | async-start | bytes 1966080 | tf_op jit(solution)/shard_map/while/body/eval_jaxpr/all_gather | solution.py:99
  2975.7 9.1 collective-permute-start.1
  (307 other events, 1925.6 us)
Sparse Core Ops, SparseCore 0:
  44.5 49.2 all-reduce.4
  106.0 45.2 all-reduce.6
  163.9 24.1 all-gather.2
  206.3 45.6 all-reduce.4
  264.0 45.3 all-reduce.6
  322.1 24.1 all-gather.2
  364.3 45.7 all-reduce.4
  422.2 45.3 all-reduce.6
  480.2 24.2 all-gather.2
  522.5 45.6 all-reduce.4
  580.4 45.2 all-reduce.6
  638.4 24.2 all-gather.2
  680.7 45.7 all-reduce.4
  738.6 45.1 all-reduce.6
  796.4 24.1 all-gather.2
  838.7 45.6 all-reduce.4
  896.5 45.2 all-reduce.6
  954.5 24.1 all-gather.2
  996.7 45.6 all-reduce.4
  1054.6 45.2 all-reduce.6
  1112.6 24.1 all-gather.2
  1154.8 45.6 all-reduce.4
  1212.7 45.2 all-reduce.6
  1270.7 24.1 all-gather.2
  1313.0 45.6 all-reduce.4
  1370.9 45.2 all-reduce.6
  1428.9 24.1 all-gather.2
  1489.1 45.7 all-reduce.8
  1556.5 45.2 all-reduce.10
  1623.1 22.6 all-gather.4
  1659.3 45.7 all-reduce.8
  1726.8 45.2 all-reduce.10
  1793.3 22.6 all-gather.4
  1829.6 45.6 all-reduce.8
  1897.0 45.2 all-reduce.10
  1963.6 22.6 all-gather.4
  1999.8 45.6 all-reduce.8
  2067.2 45.2 all-reduce.10
  2133.8 22.6 all-gather.4
  2170.0 45.7 all-reduce.8
  2237.5 45.2 all-reduce.10
  2304.1 22.6 all-gather.4
  2340.3 45.6 all-reduce.8
  2407.7 45.2 all-reduce.10
  2474.3 22.6 all-gather.4
  2510.5 45.6 all-reduce.8
  2578.0 45.2 all-reduce.10
  2644.6 22.5 all-gather.4
  2680.8 45.6 all-reduce.8
  2748.2 45.2 all-reduce.10
  2814.8 22.6 all-gather.4
  2851.0 45.6 all-reduce.8
  2918.5 45.2 all-reduce.10
  2985.0 22.6 all-gather.4
where the time goes:
time: 3030 us; the launch traced here: 3020 us
  waiting for transfers between devices  1810 us (60%)
  matrix products  580 us (19%)
  other arithmetic  423 us (14%)
  local copies, waits for them, and re-layouts  97.4 us (3%)
  starting transfers between devices  59.1 us (2%)
  loops' own time  34.8 us (1%)
    psum x9, waiting for transfers between devices, layer_forward(): attn_sum = lax.psum(attn_part, 'tp')  415 us
    psum x9, waiting for transfers between devices, layer_forward(): mlp_sum = lax.psum(mlp_part, 'tp')  408 us
    psum x9, waiting for transfers between devices, layer_backward(): lax.psum(jnp.einsum('bsf,df->bsd', g_pre_half, w_fc1, preferred_element_t...  342 us
    psum x9, waiting for transfers between devices, layer_backward(): lax.psum(jnp.einsum('bsche,cdhe->bsd', g_qkv, w_qkv, preferred_element_ty...  323 us
    all_gather x18, waiting for transfers between devices, pass_on(): return lax.all_gather(moved_part, 'tp', axis=1, tiled=True)  260 us
    reduce_sum x36, other arithmetic, layer_norm(): row_var = jnp.mean(centered * centered, axis=-1, keepdims=True)  82 us
    sub x18, matrix products, causal_attention(): attn_probs = jax.nn.softmax(scores, axis=-1).astype(jnp.bfloat16)  70.6 us
    dot_general x9, matrix products, layer_backward(): jnp.einsum('bsf,bsd->fd', gelu_out, grad_out, preferred_element_type=jnp....  64.7 us
  transfers between devices with their start and end apart: 72, of which 72 were waited for; matrix products, arithmetic and copies ran while one was open for 12% of the time, Pallas kernels for 0%

commit v1 on v0

v1 whole, which is shorter than its diff:
```python
import functools

import jax
import jax.numpy as jnp
from jax import lax
from jax.experimental import pallas as pl
from jax.experimental.pallas import tpu as pltpu
from jax.sharding import PartitionSpec as P

LN_EPS = 1e-5
F32 = jnp.float32
BF16 = jnp.bfloat16
MESH = pl.DeviceIdType.MESH
GELU_A = 0.7978845608028654
GELU_B = 0.044715
ANY = pl.BlockSpec(memory_space=pl.ANY)
VMEM = pl.BlockSpec(memory_space=pltpu.VMEM)


def dot_nn(lhs, rhs):
    return jnp.dot(lhs, rhs, preferred_element_type=F32)


def dot_nt(lhs, rhs):
    return lax.dot_general(lhs, rhs, (((1,), (1,)), ((), ())), preferred_element_type=F32)


def dot_tn(lhs, rhs):
    return lax.dot_general(lhs, rhs, (((0,), (0,)), ((), ())), preferred_element_type=F32)


def norm_stats(x_wide):
    row_mean = jnp.mean(x_wide, axis=-1, keepdims=True)
    centered = x_wide - row_mean
    row_var = jnp.mean(centered * centered, axis=-1, keepdims=True)
    inv_std = lax.rsqrt(row_var + LN_EPS)
    return centered * inv_std, inv_std


def norm_backward(x_wide, gain, grad_h):
    normed, inv_std = norm_stats(x_wide)
    g_normed = grad_h * gain
    mean_g = jnp.mean(g_normed, axis=-1, keepdims=True)
    mean_gn = jnp.mean(g_normed * normed, axis=-1, keepdims=True)
    grad_x = (g_normed - mean_g - normed * mean_gn) * inv_std
    return grad_x, jnp.sum(grad_h * normed, axis=0, keepdims=True), jnp.sum(grad_h, axis=0, keepdims=True)


def chain_kernel(stages, tp, chunk, head_dim,
                 x_first, dy_last, wq_own, wo_own, w1_own, w2_own, bias_own, bias_rep,
                 h_all, mid_all, gin_all, gmid_all, mix_all, gqkv_all, x_all, dy_all, small_out,
                 wq, wo, w1, w2, bias, x_buf, dy_buf, qkv, mix, mid, y_buf, gmid, gin, gqkv, dkv, prob, dgelu, acc, hbuf,
                 own_sem, ring_send, ring_recv, fwd_send, fwd_recv, bias_send, bias_recv,
                 hop_send, hop_recv, ag_send, ag_recv, bw_send, bw_recv, gq_send, gq_recv, out_sem, all_send, all_recv):
    stage = lax.axis_index("pp")
    me = lax.axis_index("tp")
    seq_len = x_first.shape[0]
    chunks = seq_len // chunk
    group = wo_own.shape[0]
    heads = group // head_dim
    d_model = x_first.shape[1]
    last = stages - 1
    right, left = lax.rem(me + 1, tp), lax.rem(me + tp - 1, tp)
    not_first, not_last = stage > 0, stage < last
    peers = [lax.rem(me + off, tp) for off in range(1, tp)]

    barrier = pltpu.get_barrier_semaphore()
    for peer in peers:
        pl.semaphore_signal(barrier, inc=1, device_id={"tp": peer}, device_id_type=MESH)

    @pl.when(not_first)
    def _():
        pl.semaphore_signal(barrier, inc=1, device_id={"pp": stage - 1}, device_id_type=MESH)

    @pl.when(not_last)
    def _():
        pl.semaphore_signal(barrier, inc=1, device_id={"pp": stage + 1}, device_id_type=MESH)

    pl.semaphore_wait(barrier, tp - 1 + jnp.minimum(stage, 1) + jnp.minimum(last - stage, 1))

    shards = ((wq_own, wq), (wo_own, wo), (w1_own, w1), (w2_own, w2))

    def half(ref, idx):
        size = ref.shape[0] // 2
        return ref.at[pl.ds(idx * size, size)]

    def ring_copy(w_idx, h_idx, side):
        own, full = shards[w_idx]
        target = right if side == 0 else left
        return pltpu.make_async_remote_copy(
            src_ref=half(own, h_idx), dst_ref=half(full.at[me], h_idx),
            send_sem=ring_send.at[w_idx, h_idx, side], recv_sem=ring_recv.at[w_idx, h_idx, side],
            device_id={"tp": target}, device_id_type=MESH)

    def forward_copy(w_idx, side):
        own, full = shards[w_idx]
        origin = left if side == 0 else right
        target = right if side == 0 else left
        block = half(full.at[origin], side)
        return pltpu.make_async_remote_copy(
            src_ref=block, dst_ref=block,
            send_sem=fwd_send.at[w_idx, side], recv_sem=fwd_recv.at[w_idx, side],
            device_id={"tp": target}, device_id_type=MESH)

    def bias_copy(slot):
        return pltpu.make_async_remote_copy(
            src_ref=bias_own, dst_ref=bias.at[me], send_sem=bias_send.at[slot], recv_sem=bias_recv.at[slot],
            device_id={"tp": peers[slot]}, device_id_type=MESH)

    for w_idx in range(4):
        for h_idx in range(2):
            ring_copy(w_idx, h_idx, 0).start()
            ring_copy(w_idx, 1 - h_idx, 1).start()
        if w_idx == 0:
            for slot in range(tp - 1):
                bias_copy(slot).start()
    own_copies = [pltpu.make_async_copy(own, full.at[me], own_sem.at[w_idx]) for w_idx, (own, full) in enumerate(shards)]
    own_copies.append(pltpu.make_async_copy(bias_own, bias.at[me], own_sem.at[4]))
    first_copy = pltpu.make_async_copy(x_first, x_buf, own_sem.at[5])
    last_copy = pltpu.make_async_copy(dy_last, dy_buf, own_sem.at[6])
    for own_copy in own_copies:
        own_copy.start()

    @pl.when(stage == 0)
    def _():
        first_copy.start()
        first_copy.wait()

    @pl.when(stage == last)
    def _():
        last_copy.start()
        last_copy.wait()

    qkv[...] = jnp.zeros_like(qkv)
    dkv[...] = jnp.zeros_like(dkv)
    small_out[...] = jnp.zeros_like(small_out)

    for w_idx in range(4):
        ring_copy(w_idx, 0, 0).wait_recv()
        forward_copy(w_idx, 0).start()
        ring_copy(w_idx, 1, 1).wait_recv()
        forward_copy(w_idx, 1).start()
    for own_copy in own_copies:
        own_copy.wait()
    for slot in range(tp - 1):
        bias_copy(slot).wait()
    for w_idx in range(4):
        ring_copy(w_idx, 1, 0).wait_recv()
        ring_copy(w_idx, 0, 1).wait_recv()
        forward_copy(w_idx, 0).wait()
        forward_copy(w_idx, 1).wait()
        for h_idx in range(2):
            ring_copy(w_idx, h_idx, 0).wait_send()
            ring_copy(w_idx, h_idx, 1).wait_send()

    rep = bias_rep
    lane = lax.broadcasted_iota(jnp.int32, (chunk, group), 1)
    lane_head = lane // head_dim

    def stack_heads(block):
        zero = jnp.zeros_like(block)
        return jnp.concatenate([jnp.where(lane_head == h_idx, block, zero) for h_idx in range(heads)], axis=0)

    def unstack_heads(stacked):
        total = jnp.where(lane_head == 0, stacked[:chunk], 0.0)
        for h_idx in range(1, heads):
            total = total + jnp.where(lane_head == h_idx, stacked[h_idx * chunk:(h_idx + 1) * chunk], 0.0)
        return total

    def hop_copy(c_idx, forward):
        rows = pl.ds(c_idx * chunk, chunk)
        src, dst, way, target = (y_buf, x_buf, 0, stage + 1) if forward else (gin, dy_buf, 1, stage - 1)
        return pltpu.make_async_remote_copy(
            src_ref=src.at[rows], dst_ref=dst.at[rows],
            send_sem=hop_send.at[way, c_idx], recv_sem=hop_recv.at[way, c_idx],
            device_id={"pp": target}, device_id_type=MESH)

    def fwd_chunk(c_idx, carry):
        rows = pl.ds(pl.multiple_of(c_idx * chunk, chunk), chunk)

        @pl.when(not_first)
        def _():
            hop_copy(c_idx, True).wait_recv()

        normed, _ = norm_stats(x_buf[rows, :].astype(F32))
        hbuf[...] = (normed * rep[0:1, :] + rep[1:2, :]).astype(BF16)

        @pl.loop(0, tp)
        def _(t_idx):
            for part in range(3):
                w_part = wq[t_idx, pl.ds(part * group, group), :]
                b_part = bias[t_idx, 1:2, part * group:(part + 1) * group]
                qkv[part, t_idx, rows, :] = (dot_nt(hbuf[...], w_part) + b_part).astype(BF16)

        row_pos = c_idx * chunk + lax.rem(lax.broadcasted_iota(jnp.int32, (heads * chunk, seq_len), 0), chunk)
        col_pos = lax.broadcasted_iota(jnp.int32, (heads * chunk, seq_len), 1)
        causal = row_pos >= col_pos

        @pl.loop(0, tp)
        def _(t_idx):
            scores = dot_nt(stack_heads(qkv[0, t_idx, rows, :]), qkv[1, t_idx]) * (head_dim ** -0.5)
            scores = jnp.where(causal, scores, -1e30)
            expd = jnp.exp(scores - jnp.max(scores, axis=-1, keepdims=True))
            probs = expd / jnp.sum(expd, axis=-1, keepdims=True)
            prob[c_idx, t_idx] = probs
            mix[t_idx, rows, :] = unstack_heads(dot_nn(probs.astype(BF16), qkv[2, t_idx])).astype(BF16)

        full_mix = jnp.concatenate([mix[t_idx, rows, :] for t_idx in range(tp)], axis=1)
        attn_sum = dot_nn(full_mix, wo[...].reshape(tp * group, d_model))
        x_mid = (x_buf[rows, :].astype(F32) + attn_sum + rep[4:5, :]).astype(BF16)
        mid[rows, :] = x_mid
        normed_two, _ = norm_stats(x_mid.astype(F32))
        hbuf[...] = (normed_two * rep[2:3, :] + rep[3:4, :]).astype(BF16)
        acc[...] = jnp.zeros_like(acc)

        @pl.loop(0, tp)
        def _(t_idx):
            pre = dot_nn(hbuf[...], w1[t_idx]) + bias[t_idx, 0:1, :]
            tanh = jnp.tanh(GELU_A * (pre + GELU_B * (pre * pre * pre)))
            cdf = 0.5 * (1.0 + tanh)
            dgelu[t_idx, rows, :] = cdf + 0.5 * pre * (1.0 - tanh * tanh) * (GELU_A * (1.0 + 3.0 * GELU_B * (pre * pre)))
            acc[...] += dot_nn((pre * cdf).astype(BF16), w2[t_idx])

        y_buf[rows, :] = (mid[rows, :].astype(F32) + acc[...] + rep[5:6, :]).astype(BF16)

        @pl.when(not_last)
        def _():
            hop_copy(c_idx, True).start()

        return carry

    lax.fori_loop(0, chunks, fwd_chunk, 0)

    def ag_copy(kind, slot):
        src, dst = (y_buf, h_all) if kind == 0 else (mid, mid_all)
        return pltpu.make_async_remote_copy(
            src_ref=src, dst_ref=dst.at[me], send_sem=ag_send.at[kind, slot], recv_sem=ag_recv.at[kind, slot],
            device_id={"tp": peers[slot]}, device_id_type=MESH)

    def mix_copy(slot):
        return pltpu.make_async_remote_copy(
            src_ref=mix.at[peers[slot]], dst_ref=mix_all.at[me], send_sem=ag_send.at[2, slot], recv_sem=ag_recv.at[2, slot],
            device_id={"tp": peers[slot]}, device_id_type=MESH)

    for slot in range(tp - 1):
        ag_copy(0, slot).start()
        ag_copy(1, slot).start()
        mix_copy(slot).start()
    fwd_out = [pltpu.make_async_copy(y_buf, h_all.at[me], out_sem.at[0]),
               pltpu.make_async_copy(mid, mid_all.at[me], out_sem.at[1]),
               pltpu.make_async_copy(mix.at[me], mix_all.at[me], out_sem.at[2]),
               pltpu.make_async_copy(x_buf, x_all.at[me], out_sem.at[3])]
    for out_copy in fwd_out:
        out_copy.start()

    def bw_copy(kind, c_idx, slot):
        rows = pl.ds(c_idx * chunk, chunk)
        src, dst = (gmid, gmid_all) if kind == 0 else (gin, gin_all)
        return pltpu.make_async_remote_copy(
            src_ref=src.at[rows], dst_ref=dst.at[me, rows], send_sem=bw_send.at[kind, c_idx, slot], recv_sem=bw_recv.at[kind, c_idx, slot],
            device_id={"tp": peers[slot]}, device_id_type=MESH)

    def gq_copy(c_idx, part, slot):
        rows = pl.ds(c_idx * chunk, chunk)
        return pltpu.make_async_remote_copy(
            src_ref=gqkv.at[peers[slot], part, rows], dst_ref=gqkv_all.at[me, part, rows],
            send_sem=gq_send.at[part, c_idx, slot], recv_sem=gq_recv.at[part, c_idx, slot],
            device_id={"tp": peers[slot]}, device_id_type=MESH)

    def bwd_chunk(step, carry):
        c_idx = chunks - 1 - step
        rows = pl.ds(pl.multiple_of(c_idx * chunk, chunk), chunk)

        @pl.when(not_last)
        def _():
            hop_copy(c_idx, False).wait_recv()

        acc[...] = jnp.zeros_like(acc)

        @pl.loop(0, tp)
        def _(t_idx):
            g_gelu = dot_nt(dy_buf[rows, :], w2[t_idx]).astype(BF16).astype(F32)
            g_pre = (g_gelu * dgelu[t_idx, rows, :]).astype(BF16)
            acc[...] += dot_nt(g_pre, w1[t_idx])

        g_h_two = acc[...].astype(BF16).astype(F32)
        dy_wide = dy_buf[rows, :].astype(F32)
        g_ln, g_gain, g_shift = norm_backward(mid[rows, :].astype(F32), rep[2:3, :], g_h_two)
        g_mid = (dy_wide + g_ln.astype(BF16).astype(F32)).astype(BF16)
        gmid[rows, :] = g_mid
        small_out[2:3, :] += g_gain
        small_out[3:4, :] += g_shift
        small_out[4:5, :] += jnp.sum(g_mid.astype(F32), axis=0, keepdims=True)
        small_out[5:6, :] += jnp.sum(dy_wide, axis=0, keepdims=True)
        acc[...] = jnp.zeros_like(acc)

        @pl.loop(0, tp)
        def _(t_idx):
            g_mix = dot_nt(gmid[rows, :], wo[t_idx]).astype(BF16)
            g_stack = stack_heads(g_mix)
            q_stack = stack_heads(qkv[0, t_idx, rows, :])
            probs = prob[c_idx, t_idx]
            g_prob = dot_nt(g_stack, qkv[2, t_idx]).astype(BF16).astype(F32)
            inner = jnp.sum(g_prob * probs, axis=-1, keepdims=True)
            g_score = (probs * (g_prob - inner) * (head_dim ** -0.5)).astype(BF16)
            gqkv[t_idx, 0, rows, :] = unstack_heads(dot_nn(g_score, qkv[1, t_idx])).astype(BF16)
            dkv[0, t_idx] += dot_tn(g_score, q_stack)
            dkv[1, t_idx] += dot_tn(probs.astype(BF16), g_stack)
            gqkv[t_idx, 1, rows, :] = dkv[0, t_idx, rows, :].astype(BF16)
            gqkv[t_idx, 2, rows, :] = dkv[1, t_idx, rows, :].astype(BF16)
            g_three = jnp.concatenate([gqkv[t_idx, part, rows, :] for part in range(3)], axis=1)
            acc[...] += dot_nn(g_three, wq[t_idx])

        g_h_one = acc[...].astype(BF16).astype(F32)
        g_ln_one, g_gain_one, g_shift_one = norm_backward(x_buf[rows, :].astype(F32), rep[0:1, :], g_h_one)
        gin[rows, :] = (gmid[rows, :].astype(F32) + g_ln_one.astype(BF16).astype(F32)).astype(BF16)
        small_out[0:1, :] += g_gain_one
        small_out[1:2, :] += g_shift_one

        @pl.when(not_first)
        def _():
            hop_copy(c_idx, False).start()

        for slot in range(tp - 1):
            bw_copy(1, c_idx, slot).start()
        for slot in range(tp - 1):
            bw_copy(0, c_idx, slot).start()
            for part in range(3):
                gq_copy(c_idx, part, slot).start()
        return carry

    lax.fori_loop(0, chunks, bwd_chunk, 0)

    bwd_out = [pltpu.make_async_copy(gin, gin_all.at[me], out_sem.at[4]),
               pltpu.make_async_copy(gmid, gmid_all.at[me], out_sem.at[5]),
               pltpu.make_async_copy(gqkv.at[me], gqkv_all.at[me], out_sem.at[6]),
               pltpu.make_async_copy(dy_buf, dy_all.at[me], out_sem.at[7])]
    for out_copy in bwd_out:
        out_copy.start()

    def pass_copy(way, slot):
        src, dst, target = (h_all, x_all, stage + 1) if way == 0 else (gin_all, dy_all, stage - 1)
        origin = peers[slot]
        return pltpu.make_async_remote_copy(
            src_ref=src.at[origin], dst_ref=dst.at[origin], send_sem=all_send.at[way, slot], recv_sem=all_recv.at[way, slot],
            device_id={"pp": target}, device_id_type=MESH)

    def came(make, slot):
        make(slot).wait_recv()

    for slot in range(tp - 1):
        ag_copy(0, slot).wait_recv()

    @pl.when(not_last)
    def _():
        for slot in range(tp - 1):
            pass_copy(0, slot).start()

    for slot in range(tp - 1):
        for c_idx in range(chunks):
            bw_copy(1, c_idx, slot).wait_recv()

    @pl.when(not_first)
    def _():
        for slot in range(tp - 1):
            pass_copy(1, slot).start()

    for slot in range(tp - 1):
        ag_copy(1, slot).wait_recv()
        mix_copy(slot).wait_recv()
        for kind in range(3):
            ag_copy(0 if kind == 0 else 1, slot).wait_send() if kind < 2 else mix_copy(slot).wait_send()
        for c_idx in range(chunks):
            bw_copy(0, c_idx, slot).wait()
            bw_copy(1, c_idx, slot).wait_send()
            for part in range(3):
                gq_copy(c_idx, part, slot).wait()
    for out_copy in fwd_out + bwd_out:
        out_copy.wait()

    @pl.when(not_last)
    def _():
        for c_idx in range(chunks):
            hop_copy(c_idx, True).wait_send()
        for slot in range(tp - 1):
            pass_copy(0, slot).wait_send()
            pass_copy(1, slot).wait_recv()

    @pl.when(not_first)
    def _():
        for c_idx in range(chunks):
            hop_copy(c_idx, False).wait_send()
        for slot in range(tp - 1):
            pass_copy(1, slot).wait_send()
            pass_copy(0, slot).wait_recv()


def run_chain(stages, tp, x_first, dy_last, wq, wo, w1, w2, bias_own, bias_rep, head_dim):
    seq_len, d_model = x_first.shape
    chunk = min(128, seq_len)
    chunks = seq_len // chunk
    group = wo.shape[0]
    heads = group // head_dim
    ff_local = w1.shape[1]
    rows = (tp, seq_len, d_model)
    outs = [jax.ShapeDtypeStruct(rows, BF16)] * 4
    outs += [jax.ShapeDtypeStruct((tp, seq_len, group), BF16), jax.ShapeDtypeStruct((tp, 3, seq_len, group), BF16)]
    outs += [jax.ShapeDtypeStruct(rows, BF16)] * 2 + [jax.ShapeDtypeStruct((8, d_model), F32)]
    act = pltpu.VMEM((seq_len, d_model), BF16)
    dma = pltpu.SemaphoreType.DMA
    scratch = [
        pltpu.VMEM((tp,) + wq.shape, BF16), pltpu.VMEM((tp,) + wo.shape, BF16),
        pltpu.VMEM((tp,) + w1.shape, BF16), pltpu.VMEM((tp,) + w2.shape, BF16),
        pltpu.VMEM((tp,) + bias_own.shape, F32),
        act, act,
        pltpu.VMEM((3, tp, seq_len, group), BF16), pltpu.VMEM((tp, seq_len, group), BF16),
        act, act, act, act,
        pltpu.VMEM((tp, 3, seq_len, group), BF16), pltpu.VMEM((2, tp, seq_len, group), F32),
        pltpu.VMEM((chunks, tp, heads * chunk, seq_len), F32), pltpu.VMEM((tp, seq_len, ff_local), F32),
        pltpu.VMEM((chunk, d_model), F32), pltpu.VMEM((chunk, d_model), BF16),
        dma((7,)), dma((4, 2, 2)), dma((4, 2, 2)), dma((4, 2)), dma((4, 2)), dma((tp - 1,)), dma((tp - 1,)),
        dma((2, chunks)), dma((2, chunks)), dma((3, tp - 1)), dma((3, tp - 1)),
        dma((2, chunks, tp - 1)), dma((2, chunks, tp - 1)), dma((3, chunks, tp - 1)), dma((3, chunks, tp - 1)),
        dma((8,)), dma((2, tp - 1)), dma((2, tp - 1)),
    ]
    return pl.pallas_call(
        functools.partial(chain_kernel, stages, tp, chunk, head_dim),
        out_shape=outs,
        in_specs=[ANY] * 7 + [VMEM],
        out_specs=[ANY] * 8 + [VMEM],
        scratch_shapes=scratch,
        compiler_params=pltpu.CompilerParams(collective_id=0, has_side_effects=True, vmem_limit_bytes=67043328),
        name="chain",
    )(x_first, dy_last, wq, wo, w1, w2, bias_own, bias_rep)


def layer_norm(x_act, ln_gain, ln_shift):
    normed, _ = norm_stats(x_act.astype(F32))
    return (normed * ln_gain + ln_shift).astype(BF16)


def gelu_tanh(pre_act):
    return jax.nn.gelu(pre_act, approximate=True)


def solution(mesh):
    stages = mesh.shape["pp"]
    tp = mesh.shape["tp"]

    def stage_program(x_in, dy_out, w_qkv, b_qkv, w_out, b_out, ln_par, w_fc1, b_fc1, w_fc2, b_fc2):
        micro_count, batch_rows, seq_len, d_model = x_in.shape
        head_dim = w_qkv.shape[4]
        group = w_qkv.shape[3] * head_dim
        ff_local = w_fc1.shape[2]
        seqs = micro_count * batch_rows
        stage = lax.axis_index("pp")
        me = lax.axis_index("tp")
        wq = jnp.transpose(w_qkv[0], (0, 2, 3, 1)).reshape(3 * group, d_model)
        wo = w_out[0].reshape(group, d_model)
        w1, w2 = w_fc1[0], w_fc2[0]
        bias_own = jnp.zeros((8, ff_local), F32)
        bias_own = bias_own.at[0, :].set(b_fc1[0].astype(F32)).at[1, :3 * group].set(b_qkv[0].reshape(3 * group).astype(F32))
        ln_wide = ln_par[0].astype(F32)
        bias_rep = jnp.concatenate([ln_wide, b_out.astype(F32), b_fc2.astype(F32), jnp.zeros((2, d_model), F32)], axis=0)
        x_flat = x_in.reshape(seqs, seq_len, d_model)
        dy_flat = dy_out.reshape(seqs, seq_len, d_model)
        x_first = lax.dynamic_index_in_dim(x_flat, me, 0, keepdims=False)
        dy_last = lax.dynamic_index_in_dim(dy_flat, me, 0, keepdims=False)
        h_all, mid_all, gin_all, gmid_all, mix_all, gqkv_all, x_all, dy_all, small = run_chain(
            stages, tp, x_first, dy_last, wq, wo, w1, w2, bias_own, bias_rep, head_dim)
        small = lax.psum(small, "tp")
        x_all = jnp.where(stage == 0, x_flat, x_all)
        dy_all = jnp.where(stage == stages - 1, dy_flat, dy_all)
        h_two = layer_norm(mid_all, ln_wide[2], ln_wide[3])
        pre_act = jnp.einsum("bsd,df->bsf", h_two, w1, preferred_element_type=F32) + b_fc1[0].astype(F32)
        g_gelu = jnp.einsum("bsd,fd->bsf", dy_all, w2, preferred_element_type=F32).astype(BF16)
        gelu_wide, gelu_pull = jax.vjp(gelu_tanh, pre_act)
        g_pre = gelu_pull(g_gelu.astype(F32))[0]
        g_b_fc1 = jnp.sum(g_pre, axis=(0, 1))
        g_w_fc2 = jnp.einsum("bsf,bsd->fd", gelu_wide.astype(BF16), dy_all, preferred_element_type=F32)
        g_w_fc1 = jnp.einsum("bsd,bsf->df", h_two, g_pre.astype(BF16), preferred_element_type=F32)
        g_w_out = jnp.einsum("bsf,bsd->fd", mix_all, gmid_all, preferred_element_type=F32)
        h_one = layer_norm(x_all, ln_wide[0], ln_wide[1])
        g_w_qkv = jnp.einsum("bcsf,bsd->cfd", gqkv_all, h_one, preferred_element_type=F32)
        g_w_qkv = jnp.transpose(g_w_qkv.reshape(3, group // head_dim, head_dim, d_model), (0, 3, 1, 2))
        g_b_qkv = jnp.sum(gqkv_all.astype(F32), axis=(0, 2)).reshape(3, group // head_dim, head_dim)
        shape = (micro_count, batch_rows, seq_len, d_model)
        grads = (g_w_qkv, g_b_qkv, g_w_out.reshape(group // head_dim, head_dim, d_model), small[4], small[:4], g_w_fc1, g_b_fc1, g_w_fc2, small[5])
        return (h_all.reshape(shape)[None], gin_all.reshape(shape)[None]) + tuple(g_item[None] for g_item in grads)

    act_spec = P(None, "dp", None, None)
    arg_specs = (act_spec, act_spec,
                 P("pp", None, None, "tp", None), P("pp", None, "tp", None), P("pp", "tp", None, None),
                 P("pp", None), P("pp", None, None), P("pp", None, "tp"), P("pp", "tp"),
                 P("pp", "tp", None), P("pp", None))
    stage_spec = P("pp", None, "dp", None, None)
    grad_axes = ("dp", "pp")
    result_specs = (stage_spec, stage_spec,
                    P(grad_axes, None, None, "tp", None), P(grad_axes, None, "tp", None), P(grad_axes, "tp", None, None),
                    P(grad_axes, None), P(grad_axes, None, None), P(grad_axes, None, "tp"), P(grad_axes, "tp"),
                    P(grad_axes, "tp", None), P(grad_axes, None))
    return jax.shard_map(stage_program, mesh=mesh, in_specs=arg_specs, out_specs=result_specs, check_vma=False)
```

time: 3030 us -> 636 us (0.21)
  the two profiles are of different devices: /device:TPU:97 before, /device:TPU:96 now
where the time goes in v1:
time: 636 us; the launch traced here: 635 us
  Pallas kernels  561 us (88%)
  matrix products  32.7 us (5%)
  blocking collectives  14.7 us (2%)
  local copies, waits for them, and re-layouts  13 us (2%)
  other arithmetic  13 us (2%)
    pallas_call x1, Pallas kernels, run_chain(): pl.pallas_call(functools.partial(chain_kernel, stages, tp, chunk, head_di...  561 us
    psum x1, blocking collectives, stage_program(): small = lax.psum(small, 'tp')  14.7 us

profile of v1, /device:TPU:96, one launch (start us, length us, event | category | flops | bytes accessed | tf_op | source)
XLA Modules:
  0.0 635.3 jit_solution(1360429837417253521)
XLA Ops:
  0.7 0.1 pad.10.clone
  0.7 0.8 reshape.144
  1.5 0.7 convert_element_type.66
  2.2 0.7 convert_element_type.67
  2.9 1.3 convert_element_type.80
  4.2 0.7 convert_bitcast_fusion
  4.9 0.7 maximum_maximum_fusion.bias_rep
  5.6 1.5 fusion.45
  7.0 1.3 pad_convert_fusion
  8.3 1.4 scatter.14.bias_own
  9.7 2.6 dynamic-slice_bitcast_fusion
  12.3 561.2 %chain.1 = (bf16[4,384,1024]{2,1,0:T(8,128)(2,1)}, bf16[4,384,1024]{2,1,0:T(8,128)(2,1)}, bf16[4,384,1024]{2,1,0:T(8,128)(2,1)}, bf16[4,384,1024]{2,1,0:T(8,128)...) custom-call(bf16[384,1024]{1,0:T(8,128)(2,1)} %get-tuple-element.64., ...), custom_call_target="tpu_custom_call" | custom-call | tf_op jit(solution)/shard_map/chain/pallas_call | solution.py:426
  573.5 0.0 copy-start
  573.5 0.0 copy-start.9
  573.6 2.2 convert_reduce_fusion.2
  575.7 0.7 broadcast_in_dim_reshape.14
  576.4 2.4 convert_reduce_fusion
  578.8 0.0 copy-done
  578.8 1.0 fusion.4
  579.8 0.0 copy-done.9
  579.8 14.7 %psum.7 = f32[8,1024]{1,0:T(8,128)S(1)} all-reduce(f32[8,1024]{1,0:T(8,128)S(1)} %copy-done.9), channel_id=1, replica_groups=mesh['dp'=1,'tp'=4,'pp'=8] {'tp'}, use_global_device_ids=true, to_apply=%region_3.4 | all-reduce | flops 8192 | bytes 65536 | tf_op jit(solution)/shard_map/psum | solution.py:471
  594.5 0.0 copy-start.1
  594.5 0.0 copy-start.2
  594.5 0.6 fusion.44
  595.1 0.6 slice_bitcast_fusion
  595.7 4.7 fusion.47
  600.4 0.0 copy-done.1
  600.4 0.0 copy-done.2
  600.4 0.0 copy-start.5
  600.4 0.0 copy-start.13
  600.5 0.0 copy-start.14
  600.5 1.0 convert_reduce_fusion.1
  601.5 1.0 fusion.8
  602.5 0.0 copy-done.5
  602.5 0.0 copy-done.13
  602.5 0.0 copy-done.14
  602.5 0.0 copy-start.6
  602.6 0.0 copy-start.11
  602.6 0.0 copy-start.12
  602.6 4.6 fusion.22
  607.2 0.0 copy-done.6
  607.2 0.0 copy-done.11
  607.2 0.0 copy-done.12
  607.2 0.0 copy-start.7
  607.2 0.0 copy-start.8
  607.2 0.0 copy-start.10
  607.3 0.0 copy-start.15
  607.3 3.8 fusion.35
  611.0 0.0 copy-done.7
  611.1 0.0 copy-done.8
  611.1 0.0 copy-done.10
  611.1 0.0 copy-done.15
  611.1 8.3 %fusion.46 = (f32[1024]{0:T(1024)}, bf16[4,384,1024]{2,1,0:T(8,128)(2,1)S(1)}) fusion(f32[4,384,1024]{2,1,0:T(8,128)S(1)} %fusion.35, f32[1024]{0:T(1024)S(1)} %bitcast.72, bf16[1,1024,1024]{2,1,0:T(8,128)(2,1)S(1)} %copy-done.7, bf16[4,384,1024]{2,1,0:T(8,128)(2,1)S(1)} %bitcast.70, bf16[4,384,1024]{2,1,0:T(8,128)(2,1)S(1)} %copy-done.15, pred[]{:T(512)S(6)} %eq.7), kind=kOutput, calls=%fused_computation.63 | convolution fusion | flops 3260546048 | bytes 17833984 | tf_op jit(solution)/shard_map/bsd,fd->bsf/dot_general | solution.py:476
  619.4 5.4 fusion.31
  624.8 0.0 copy-start.4
  624.8 5.9 fusion.32
  630.6 0.0 copy-done.4
  630.6 0.0 copy-start.3
  630.6 1.7 copy.34
  632.3 1.4 copy-done.3
  633.7 1.7 copy.35
  (5 shorter events, 0.0 us)
Async XLA Ops:
  573.5 5.3 copy-start
  573.5 6.3 copy-start.9
  594.5 5.9 copy-start.1
  594.5 5.9 copy-start.2
  600.4 2.1 copy-start.5
  600.4 2.1 copy-start.13
  600.5 2.1 copy-start.14
  602.5 4.7 copy-start.6
  602.6 4.7 copy-start.11
  602.6 4.7 copy-start.12
  607.2 3.8 copy-start.7
  607.2 3.8 copy-start.8
  607.2 3.8 copy-start.10
  607.3 3.8 copy-start.15
  624.8 5.9 copy-start.4
  630.6 3.0 copy-start.3

commit v2 on v1

v2 whole, which is shorter than its diff:
```python
import functools

import jax
import jax.numpy as jnp
from jax import lax
from jax.experimental import pallas as pl
from jax.experimental.pallas import tpu as pltpu
from jax.sharding import PartitionSpec as P

LN_EPS = 1e-5
F32 = jnp.float32
BF16 = jnp.bfloat16
MESH = pl.DeviceIdType.MESH
GELU_A = 0.7978845608028654
GELU_B = 0.044715
LOG2_E = 1.4426950408889634
ANY = pl.BlockSpec(memory_space=pl.ANY)
VMEM = pl.BlockSpec(memory_space=pltpu.VMEM)


def dot_nn(lhs, rhs):
    return jnp.dot(lhs, rhs, preferred_element_type=F32)


def dot_nt(lhs, rhs):
    return lax.dot_general(lhs, rhs, (((1,), (1,)), ((), ())), preferred_element_type=F32)


def dot_tn(lhs, rhs):
    return lax.dot_general(lhs, rhs, (((0,), (0,)), ((), ())), preferred_element_type=F32)


def norm_stats(x_wide):
    row_mean = jnp.mean(x_wide, axis=-1, keepdims=True)
    centered = x_wide - row_mean
    row_var = jnp.mean(centered * centered, axis=-1, keepdims=True)
    inv_std = lax.rsqrt(row_var + LN_EPS)
    return centered * inv_std, inv_std


def norm_backward(x_wide, gain, grad_h):
    normed, inv_std = norm_stats(x_wide)
    g_normed = grad_h * gain
    mean_g = jnp.mean(g_normed, axis=-1, keepdims=True)
    mean_gn = jnp.mean(g_normed * normed, axis=-1, keepdims=True)
    grad_x = (g_normed - mean_g - normed * mean_gn) * inv_std
    return grad_x, jnp.sum(grad_h * normed, axis=0, keepdims=True), jnp.sum(grad_h, axis=0, keepdims=True)


def gelu_parts(pre):
    square = pre * pre
    tanh = jnp.tanh(pre * (GELU_A + (GELU_A * GELU_B) * square))
    cdf = 0.5 + 0.5 * tanh
    return cdf, cdf + pre * (0.5 * GELU_A + (1.5 * GELU_A * GELU_B) * square) * (1.0 - tanh * tanh)


def chain_kernel(stages, tp, chunk, head_dim,
                 x_flat, dy_flat, wq_own, wo_own, w1_own, w2_own, params,
                 h_all, mid_all, gin_all, gmid_all, mix_all, gqkv_all, x_all, dy_all, h_one_all, h_two_all, act_all, gpre_all, slope_all, small_out,
                 wq, wq_t, wo, w1, w2, bias, x_buf, dy_buf, qkv, mix, mid, y_buf, gmid, gin, dkv, prob, dgelu, acc, hbuf, small,
                 own_sem, go_sem, done_sem, ring_send, ring_recv, fwd_send, fwd_recv, bias_send, bias_recv,
                 hop_send, hop_recv, ag_send, ag_recv, mix_send, mix_recv, bw_send, bw_recv, gq_send, gq_recv,
                 out_sem, px_send, px_recv, py_send, py_recv, sum_send, sum_recv, prep_sem, post_sem):
    stage = lax.axis_index("pp")
    me = lax.axis_index("tp")
    seq_len, d_model = x_buf.shape
    chunks = seq_len // chunk
    group = wo_own.shape[0]
    heads = group // head_dim
    last = stages - 1
    right, left = lax.rem(me + 1, tp), lax.rem(me + tp - 1, tp)
    not_first, not_last = stage > 0, stage < last
    peers = [lax.rem(me + off, tp) for off in range(1, tp)]
    even = lax.rem(stage, 2) == 0
    score_scale = head_dim ** -0.5

    def remote(src, dst, send, recv, axis, target):
        return pltpu.make_async_remote_copy(src_ref=src, dst_ref=dst, send_sem=send, recv_sem=recv,
                                            device_id={axis: target}, device_id_type=MESH)

    small[...] = jnp.zeros_like(small)
    small_out[...] = jnp.zeros_like(small_out)
    barrier = pltpu.get_barrier_semaphore()
    for peer in peers:
        pl.semaphore_signal(barrier, inc=1, device_id={"tp": peer}, device_id_type=MESH)

    @pl.when(not_first)
    def _():
        pl.semaphore_signal(barrier, inc=1, device_id={"pp": stage - 1}, device_id_type=MESH)

    @pl.when(not_last)
    def _():
        pl.semaphore_signal(barrier, inc=1, device_id={"pp": stage + 1}, device_id_type=MESH)

    pl.semaphore_wait(barrier, tp - 1 + jnp.minimum(stage, 1) + jnp.minimum(last - stage, 1))

    def shard(w_idx, origin):
        if w_idx == 1:
            return wo.at[pl.ds(pl.multiple_of(origin * group, group), group)]
        return (wq, None, w1, w2)[w_idx].at[origin]

    owns = (wq_own, wo_own, w1_own, w2_own)

    def half(ref, idx):
        size = ref.shape[0] // 2
        return ref.at[pl.ds(idx * size, size)]

    def ring_copy(w_idx, h_idx, side):
        return remote(half(owns[w_idx], h_idx), half(shard(w_idx, me), h_idx),
                      ring_send.at[w_idx, h_idx, side], ring_recv.at[w_idx, h_idx, side], "tp", left if side else right)

    def forward_copy(w_idx, side):
        block = half(shard(w_idx, right if side else left), side)
        return remote(block, block, fwd_send.at[w_idx, side], fwd_recv.at[w_idx, side], "tp", left if side else right)

    def bias_copy(slot):
        return remote(params.at[pl.ds(0, 8)], bias.at[me], bias_send.at[slot], bias_recv.at[slot], "tp", peers[slot])

    own_copies = [pltpu.make_async_copy(owns[w_idx], shard(w_idx, me), own_sem.at[w_idx]) for w_idx in range(4)]
    own_copies.append(pltpu.make_async_copy(params.at[pl.ds(0, 8)], bias.at[me], own_sem.at[4]))
    for own_copy in own_copies:
        own_copy.start()
    for slot in range(tp - 1):
        bias_copy(slot).start()

    def own_input(src, buf, dst):
        bounce = (y_buf, mid, gmid)
        copies = [pltpu.make_async_copy(src.at[me], buf, own_sem.at[5])]
        copies += [pltpu.make_async_copy(src.at[peers[slot]], bounce[slot], own_sem.at[6 + slot]) for slot in range(tp - 1)]
        for copy in copies:
            copy.start()
        for copy in copies:
            copy.wait()
        copies = [pltpu.make_async_copy(bounce[slot], dst.at[peers[slot]], own_sem.at[6 + slot]) for slot in range(tp - 1)]
        for copy in copies:
            copy.start()
        for copy in copies:
            copy.wait()

    @pl.when(jnp.logical_not(even))
    def _():
        pl.semaphore_wait(go_sem, 1)

    for w_idx in range(4):
        for h_idx in range(2):
            ring_copy(w_idx, h_idx, 0).start()
            ring_copy(w_idx, 1 - h_idx, 1).start()

    @pl.when(stage == 0)
    def _():
        own_input(x_flat, x_buf, x_all)

    @pl.when(stage == last)
    def _():
        own_input(dy_flat, dy_buf, dy_all)

    qkv[...] = jnp.zeros_like(qkv)
    dkv[...] = jnp.zeros_like(dkv)

    for w_idx in range(4):
        ring_copy(w_idx, 0, 0).wait_recv()
        forward_copy(w_idx, 0).start()
        ring_copy(w_idx, 1, 1).wait_recv()
        forward_copy(w_idx, 1).start()
    for own_copy in own_copies:
        own_copy.wait()
    for slot in range(tp - 1):
        bias_copy(slot).wait()
    for w_idx in range(4):
        ring_copy(w_idx, 1, 0).wait_recv()
        ring_copy(w_idx, 0, 1).wait_recv()
        forward_copy(w_idx, 0).wait()
        forward_copy(w_idx, 1).wait()
        for h_idx in range(2):
            ring_copy(w_idx, h_idx, 0).wait_send()
            ring_copy(w_idx, h_idx, 1).wait_send()
        if w_idx == 0:
            @pl.loop(0, tp)
            def _(t_idx):
                for part in range(3):
                    wq_t[t_idx, :, part * group:(part + 1) * group] = wq[t_idx, part * group:(part + 1) * group, :].T

    @pl.when(even)
    def _():
        pl.semaphore_signal(go_sem, inc=1, device_id={"pp": stage + 1}, device_id_type=MESH)

    @pl.when(jnp.logical_not(even))
    def _():
        pl.semaphore_signal(done_sem, inc=1, device_id={"pp": stage - 1}, device_id_type=MESH)

    rep = params.at[pl.ds(8, 8)]
    lane_head = lax.broadcasted_iota(jnp.int32, (chunk, group), 1) // head_dim

    def stack_heads(block):
        zero = jnp.zeros_like(block)
        return jnp.concatenate([jnp.where(lane_head == h_idx, block, zero) for h_idx in range(heads)], axis=0)

    def unstack_heads(stacked):
        total = stacked[:chunk]
        for h_idx in range(1, heads):
            total = jnp.where(lane_head == h_idx, stacked[h_idx * chunk:(h_idx + 1) * chunk], total)
        return total

    def hop_copy(c_idx, forward):
        rows = pl.ds(c_idx * chunk, chunk)
        src, dst, way, target = (y_buf, x_buf, 0, stage + 1) if forward else (gin, dy_buf, 1, stage - 1)
        return remote(src.at[rows], dst.at[rows], hop_send.at[way, c_idx], hop_recv.at[way, c_idx], "pp", target)

    def fwd_chunk(c_idx, carry):
        rows = pl.ds(pl.multiple_of(c_idx * chunk, chunk), chunk)

        @pl.when(not_first)
        def _():
            hop_copy(c_idx, True).wait_recv()

        normed, _ = norm_stats(x_buf[rows, :].astype(F32))
        hbuf[...] = (normed * rep[0:1, :] + rep[1:2, :]).astype(BF16)

        groups = range(tp)
        for t_idx in groups:
            pre = dot_nn(hbuf[...], wq_t[t_idx]) + bias[t_idx, 1:2, :3 * group]
            for part in range(3):
                qkv[part, t_idx, rows, :] = pre[:, part * group:(part + 1) * group].astype(BF16)

        row_pos = c_idx * chunk + lax.rem(lax.broadcasted_iota(jnp.int32, (heads * chunk, seq_len), 0), chunk)
        causal = row_pos >= lax.broadcasted_iota(jnp.int32, (heads * chunk, seq_len), 1)
        all_scores = [dot_nt(stack_heads(qkv[0, t_idx, rows, :]), qkv[1, t_idx]) for t_idx in groups]
        all_probs = []
        for t_idx in groups:
            scores = jnp.where(causal, all_scores[t_idx], -1e30)
            expd = jnp.exp2((scores - jnp.max(scores, axis=-1, keepdims=True)) * (score_scale * LOG2_E))
            probs = expd * (1.0 / jnp.sum(expd, axis=-1, keepdims=True))
            prob[c_idx, t_idx] = probs
            all_probs.append(probs.astype(BF16))
        for t_idx in groups:
            mix[t_idx, rows, :] = unstack_heads(dot_nn(all_probs[t_idx], qkv[2, t_idx])).astype(BF16)

        full_mix = jnp.concatenate([mix[t_idx, rows, :] for t_idx in groups], axis=1)
        x_mid = (x_buf[rows, :].astype(F32) + dot_nn(full_mix, wo[...]) + rep[4:5, :]).astype(BF16)
        mid[rows, :] = x_mid
        normed_two, _ = norm_stats(x_mid.astype(F32))
        hbuf[...] = (normed_two * rep[2:3, :] + rep[3:4, :]).astype(BF16)
        total = jnp.zeros((chunk, d_model), F32)
        for t_idx in groups:
            pre = dot_nn(hbuf[...], w1[t_idx]) + bias[t_idx, 0:1, :]
            cdf, slope = gelu_parts(pre)
            dgelu[t_idx, rows, :] = slope
            total = total + dot_nn((pre * cdf).astype(BF16), w2[t_idx])

        y_buf[rows, :] = (mid[rows, :].astype(F32) + total + rep[5:6, :]).astype(BF16)

        @pl.when(not_last)
        def _():
            hop_copy(c_idx, True).start()

        return carry

    lax.fori_loop(0, chunks, fwd_chunk, 0)

    def ag_copy(kind, side):
        src, dst = ((y_buf, h_all), (mid, mid_all), (gmid, gmid_all))[kind]
        return remote(src, dst.at[me], ag_send.at[kind, side], ag_recv.at[kind, side], "tp", left if side else right)

    def ag_forward(kind, side):
        rows = pl.ds(side * (seq_len // 2), seq_len // 2)
        block = (h_all, mid_all, gmid_all)[kind].at[right if side else left, rows]
        return remote(block, block, ag_send.at[kind, 2 + side], ag_recv.at[kind, 2 + side], "tp", left if side else right)

    def mix_copy(slot):
        return remote(mix.at[peers[slot]], mix_all.at[me], mix_send.at[slot], mix_recv.at[slot], "tp", peers[slot])

    def start_fwd_gather():
        for kind in range(2):
            for side in range(2):
                ag_copy(kind, side).start()
        for slot in range(tp - 1):
            mix_copy(slot).start()

    @pl.when(jnp.logical_not(even))
    def _():
        start_fwd_gather()

    fwd_out = [pltpu.make_async_copy(y_buf, h_all.at[me], out_sem.at[0]),
               pltpu.make_async_copy(mid, mid_all.at[me], out_sem.at[1]),
               pltpu.make_async_copy(mix.at[me], mix_all.at[me], out_sem.at[2]),
               pltpu.make_async_copy(x_buf, x_all.at[me], out_sem.at[3])]
    for out_copy in fwd_out:
        out_copy.start()

    def pass_x(slot):
        origin = peers[slot]
        return remote(h_all.at[origin], x_all.at[origin], px_send.at[slot], px_recv.at[slot], "pp", stage + 1)

    def finish_fwd_gather():
        for kind in range(2):
            for side in range(2):
                ag_copy(kind, side).wait_recv()
                ag_forward(kind, side).start()
        for kind in range(2):
            for side in range(2):
                ag_forward(kind, side).wait_recv()

        @pl.when(not_last)
        def _():
            for slot in range(tp - 1):
                pass_x(slot).start()

    size = group

    def flip(ref_get, ref_set, count):
        for row in range(count):
            ref_set(row, row, ref_get(row, row).T)
            for col in range(row):
                upper, lower = ref_get(col, row).T, ref_get(row, col).T
                ref_set(row, col, upper)
                ref_set(col, row, lower)

    def tile(row, col):
        return slice(row * size, (row + 1) * size), slice(col * size, (col + 1) * size)

    @pl.loop(0, tp)
    def _(t_idx):
        for ref in (w2, w1):
            def ref_set(row, col, value, ref=ref):
                ref[(t_idx,) + tile(row, col)] = value

            flip(lambda row, col, ref=ref: ref[(t_idx,) + tile(row, col)], ref_set, d_model // size)

    def wo_set(row, col, value):
        wo[tile(row, col)] = value

    flip(lambda row, col: wo[tile(row, col)], wo_set, d_model // size)

    @pl.when(even)
    def _():
        pl.semaphore_wait(done_sem, 1)
        start_fwd_gather()

    @pl.when(stage < stages // 2)
    def _():
        finish_fwd_gather()

    def bw_copy(c_idx, side):
        rows = pl.ds(c_idx * chunk, chunk)
        return remote(gin.at[rows], gin_all.at[me, rows], bw_send.at[c_idx, side], bw_recv.at[c_idx, side], "tp", left if side else right)

    def bw_forward(c_idx, side):
        rows = pl.ds(c_idx * chunk + side * (chunk // 2), chunk // 2)
        block = gin_all.at[right if side else left, rows]
        return remote(block, block, bw_send.at[c_idx, 2 + side], bw_recv.at[c_idx, 2 + side], "tp", left if side else right)

    def gqkv_of(t_idx):
        return wq_t.at[t_idx, pl.ds(0, seq_len)]

    def gq_copy(slot):
        return remote(gqkv_of(peers[slot]), gqkv_all.at[me], gq_send.at[slot], gq_recv.at[slot], "tp", peers[slot])

    def pass_dy(c_idx, slot):
        rows = pl.ds(c_idx * chunk, chunk)
        origin = peers[slot]
        return remote(gin_all.at[origin, rows], dy_all.at[origin, rows], py_send.at[c_idx, slot], py_recv.at[c_idx, slot], "pp", stage - 1)

    def forward_chunk(c_idx):
        for side in range(2):
            bw_copy(c_idx, side).wait_recv()
            bw_forward(c_idx, side).start()

    def pass_chunk(c_idx):
        for side in range(2):
            bw_forward(c_idx, side).wait_recv()

        @pl.when(not_first)
        def _():
            for slot in range(tp - 1):
                pass_dy(c_idx, slot).start()

    w1_own_t, w2_own_t = w1.at[me], w2.at[me]
    early = stage < stages // 2 - 1

    def prep(two_buf, one_buf, act_buf, keep_slopes):
        @pl.when(not_first)
        def _():
            for slot in range(tp - 1):
                pass_x(slot).wait_recv()

        def prep_seq(t_idx, carry):
            loads = [pltpu.make_async_copy(mid_all.at[t_idx], two_buf, prep_sem.at[0]), pltpu.make_async_copy(x_all.at[t_idx], one_buf, prep_sem.at[1])]
            for load in loads:
                load.start()
            for load in loads:
                load.wait()

            def prep_rows(c_idx, inner):
                rows = pl.ds(pl.multiple_of(c_idx * chunk, chunk), chunk)
                normed, _ = norm_stats(two_buf[rows, :].astype(F32))
                two_buf[rows, :] = (normed * rep[2:3, :] + rep[3:4, :]).astype(BF16)
                normed_one, _ = norm_stats(one_buf[rows, :].astype(F32))
                one_buf[rows, :] = (normed_one * rep[0:1, :] + rep[1:2, :]).astype(BF16)
                pre = dot_nt(two_buf[rows, :], w1_own_t[...]) + bias[me, 0:1, :]
                cdf, slope = gelu_parts(pre)
                act_buf[rows, :] = (pre * cdf).astype(BF16)
                if keep_slopes:
                    keep = pltpu.make_async_copy(acc, slope_all.at[t_idx, rows], prep_sem.at[2])

                    @pl.when(c_idx > 0)
                    def _():
                        keep.wait()

                    acc[...] = slope
                    keep.start()
                else:
                    dgelu[t_idx, rows, :] = slope
                return inner

            lax.fori_loop(0, chunks, prep_rows, 0)
            if keep_slopes:
                pltpu.make_async_copy(acc, slope_all.at[t_idx, pl.ds(0, chunk)], prep_sem.at[2]).wait()
            keeps = [pltpu.make_async_copy(two_buf, h_two_all.at[t_idx], prep_sem.at[0]), pltpu.make_async_copy(one_buf, h_one_all.at[t_idx], prep_sem.at[1]),
                     pltpu.make_async_copy(act_buf, act_all.at[t_idx], prep_sem.at[2])]
            for keep in keeps:
                keep.start()
            for keep in keeps:
                keep.wait()
            return carry

        lax.fori_loop(0, tp, prep_seq, 0)

    def end_fwd_sends():
        for kind in range(2):
            for side in range(2):
                ag_copy(kind, side).wait_send()
        for slot in range(tp - 1):
            mix_copy(slot).wait_send()
        for out_copy in fwd_out:
            out_copy.wait()

        @pl.when(not_last)
        def _():
            for c_idx in range(chunks):
                hop_copy(c_idx, True).wait_send()

    @pl.when(early)
    def _():
        end_fwd_sends()
        prep(gmid, gin, y_buf, True)

    def bwd_chunk(step, carry):
        c_idx = chunks - 1 - step
        rows = pl.ds(pl.multiple_of(c_idx * chunk, chunk), chunk)

        @pl.when(not_last)
        def _():
            hop_copy(c_idx, False).wait_recv()

        groups = range(tp)
        g_h_sum = jnp.zeros((chunk, d_model), F32)
        for t_idx in groups:
            g_gelu = dot_nn(dy_buf[rows, :], w2[t_idx]).astype(BF16).astype(F32)
            g_h_sum = g_h_sum + dot_nn((g_gelu * dgelu[t_idx, rows, :]).astype(BF16), w1[t_idx])

        g_h_two = g_h_sum.astype(BF16).astype(F32)
        dy_wide = dy_buf[rows, :].astype(F32)
        g_ln, g_gain, g_shift = norm_backward(mid[rows, :].astype(F32), rep[2:3, :], g_h_two)
        g_mid = (dy_wide + g_ln.astype(BF16).astype(F32)).astype(BF16)
        gmid[rows, :] = g_mid
        small[me, 2:3, :] += g_gain
        small[me, 3:4, :] += g_shift
        small[me, 4:5, :] += jnp.sum(g_mid.astype(F32), axis=0, keepdims=True)
        small[me, 5:6, :] += jnp.sum(dy_wide, axis=0, keepdims=True)
        g_mix_all = dot_nn(gmid[rows, :], wo[...]).astype(BF16)
        g_stacks = [stack_heads(g_mix_all[:, t_idx * group:(t_idx + 1) * group]) for t_idx in groups]
        g_probs = [dot_nt(g_stacks[t_idx], qkv[2, t_idx]).astype(BF16).astype(F32) for t_idx in groups]
        g_values = [dot_tn(prob[c_idx, t_idx].astype(BF16), g_stacks[t_idx]) for t_idx in groups]
        g_scores = []
        for t_idx in groups:
            probs = prob[c_idx, t_idx]
            inner = jnp.sum(g_probs[t_idx] * probs, axis=-1, keepdims=True)
            g_scores.append((probs * (g_probs[t_idx] - inner)).astype(BF16))
            dkv[1, t_idx] += g_values[t_idx]
        for t_idx in groups:
            wq_t[t_idx, rows, 0:group] = (unstack_heads(dot_nn(g_scores[t_idx], qkv[1, t_idx])) * score_scale).astype(BF16)
            dkv[0, t_idx] += dot_tn(g_scores[t_idx], stack_heads(qkv[0, t_idx, rows, :])) * score_scale
        g_h_sum = jnp.zeros((chunk, d_model), F32)
        for t_idx in groups:
            wq_t[t_idx, rows, group:2 * group] = dkv[0, t_idx, rows, :].astype(BF16)
            wq_t[t_idx, rows, 2 * group:3 * group] = dkv[1, t_idx, rows, :].astype(BF16)
            g_h_sum = g_h_sum + dot_nn(wq_t[t_idx, rows, :], wq[t_idx])

        g_h_one = g_h_sum.astype(BF16).astype(F32)
        g_ln_one, g_gain_one, g_shift_one = norm_backward(x_buf[rows, :].astype(F32), rep[0:1, :], g_h_one)
        gin[rows, :] = (gmid[rows, :].astype(F32) + g_ln_one.astype(BF16).astype(F32)).astype(BF16)
        small[me, 0:1, :] += g_gain_one
        small[me, 1:2, :] += g_shift_one

        @pl.when(not_first)
        def _():
            hop_copy(c_idx, False).start()

        for side in range(2):
            bw_copy(c_idx, side).start()

        @pl.when((step >= 2) & (stage < last - 1))
        def _():
            forward_chunk(c_idx + 2)

        return carry

    lax.fori_loop(0, chunks, bwd_chunk, 0)

    def sum_copy(slot):
        return remote(small.at[me], small.at[me], sum_send.at[slot], sum_recv.at[slot], "tp", peers[slot])

    for slot in range(tp - 1):
        sum_copy(slot).start()
    bwd_out = [pltpu.make_async_copy(gin, gin_all.at[me], out_sem.at[4]),
               pltpu.make_async_copy(gmid, gmid_all.at[me], out_sem.at[5]),
               pltpu.make_async_copy(gqkv_of(me), gqkv_all.at[me], out_sem.at[6]),
               pltpu.make_async_copy(dy_buf, dy_all.at[me], out_sem.at[7])]
    for out_copy in bwd_out:
        out_copy.start()

    @pl.when(stage >= last - 1)
    def _():
        forward_chunk(chunks - 1)

    for c_idx in range(chunks - 2, -1, -1):
        forward_chunk(c_idx)

    @pl.when(stage >= stages // 2)
    def _():
        finish_fwd_gather()

    for side in range(2):
        ag_copy(2, side).start()
    for slot in range(tp - 1):
        gq_copy(slot).start()
    for c_idx in range(chunks - 1, -1, -1):
        pass_chunk(c_idx)

    @pl.when(early)
    def _():
        slopes = pltpu.make_async_copy(slope_all, dgelu, prep_sem.at[0])
        slopes.start()
        slopes.wait()

    @pl.when(jnp.logical_not(early))
    def _():
        end_fwd_sends()
        prep(mid, x_buf, y_buf, False)

    def finish_rows(t_idx, src, dst, rows):
        grad = dot_nn(src[rows, :], w2_own_t[...]).astype(BF16).astype(F32) * dgelu[t_idx, rows, :]
        small_out[6:7, :] += jnp.sum(grad, axis=0, keepdims=True)
        dst[rows, :] = grad.astype(BF16)

    def finish_own(c_idx, carry):
        finish_rows(me, dy_buf, y_buf, pl.ds(pl.multiple_of(c_idx * chunk, chunk), chunk))
        return carry

    lax.fori_loop(0, chunks, finish_own, 0)
    own_keep = pltpu.make_async_copy(y_buf, gpre_all.at[me], prep_sem.at[0])
    own_keep.start()
    for side in range(2):
        ag_copy(2, side).wait_recv()
        ag_forward(2, side).start()
    own_keep.wait()

    def finish_peers(step, carry):
        c_idx = chunks - 1 - step
        rows = pl.ds(pl.multiple_of(c_idx * chunk, chunk), chunk)
        bufs = (x_buf, mid, y_buf)

        @pl.when(not_last)
        def _():
            for slot in range(tp - 1):
                pass_dy(c_idx, slot).wait_recv()

        loads = [pltpu.make_async_copy(dy_all.at[peers[slot], rows], bufs[slot].at[rows], post_sem.at[slot]) for slot in range(tp - 1)]
        keeps = [pltpu.make_async_copy(bufs[slot].at[rows], gpre_all.at[peers[slot], rows], post_sem.at[slot]) for slot in range(tp - 1)]
        for load in loads:
            load.start()
        for slot in range(tp - 1):
            loads[slot].wait()
            finish_rows(peers[slot], bufs[slot], bufs[slot], rows)
            keeps[slot].start()
        for keep in keeps:
            keep.wait()
        return carry

    lax.fori_loop(0, chunks, finish_peers, 0)
    for slot in range(tp - 1):
        sum_copy(slot).wait()
    total_small = small[0, 0:6, :]
    for t_idx in range(1, tp):
        total_small = total_small + small[t_idx, 0:6, :]
    small_out[0:6, :] = total_small

    for slot in range(tp - 1):
        mix_copy(slot).wait_recv()
        gq_copy(slot).wait()
    for side in range(2):
        for kind in range(3):
            ag_forward(kind, side).wait_send()
        ag_copy(2, side).wait_send()
        ag_forward(2, side).wait_recv()
        for c_idx in range(chunks):
            bw_copy(c_idx, side).wait_send()
            bw_forward(c_idx, side).wait_send()
    for out_copy in bwd_out:
        out_copy.wait()

    @pl.when(not_last)
    def _():
        for slot in range(tp - 1):
            pass_x(slot).wait_send()

    @pl.when(not_first)
    def _():
        for c_idx in range(chunks):
            hop_copy(c_idx, False).wait_send()
            for slot in range(tp - 1):
                pass_dy(c_idx, slot).wait_send()


def run_chain(stages, tp, x_flat, dy_flat, wq, wo, w1, w2, params, head_dim):
    _, seq_len, d_model = x_flat.shape
    chunk = min(128, seq_len)
    chunks = seq_len // chunk
    group = wo.shape[0]
    heads = group // head_dim
    ff_local = w1.shape[1]
    rows = (tp, seq_len, d_model)
    outs = [jax.ShapeDtypeStruct(rows, BF16)] * 4
    outs += [jax.ShapeDtypeStruct((tp, seq_len, group), BF16), jax.ShapeDtypeStruct((tp, seq_len, 3 * group), BF16)]
    outs += [jax.ShapeDtypeStruct(rows, BF16)] * 4 + [jax.ShapeDtypeStruct((tp, seq_len, ff_local), BF16)] * 2
    outs += [jax.ShapeDtypeStruct((tp, seq_len, ff_local), F32), jax.ShapeDtypeStruct((8, d_model), F32)]
    act = pltpu.VMEM((seq_len, d_model), BF16)
    dma = pltpu.SemaphoreType.DMA
    scratch = [
        pltpu.VMEM((tp,) + wq.shape, BF16), pltpu.VMEM((tp,) + wq.shape[::-1], BF16), pltpu.VMEM((tp * group, d_model), BF16),
        pltpu.VMEM((tp,) + w1.shape, BF16), pltpu.VMEM((tp,) + w2.shape, BF16),
        pltpu.VMEM((tp, 8, d_model), F32),
        act, act,
        pltpu.VMEM((3, tp, seq_len, group), BF16), pltpu.VMEM((tp, seq_len, group), BF16),
        act, act, act, act,
        pltpu.VMEM((2, tp, seq_len, group), F32),
        pltpu.VMEM((chunks, tp, heads * chunk, seq_len), F32), pltpu.VMEM((tp, seq_len, ff_local), F32),
        pltpu.VMEM((chunk, d_model), F32), pltpu.VMEM((chunk, d_model), BF16), pltpu.VMEM((tp, 8, d_model), F32),
        dma((9,)), pltpu.SemaphoreType.REGULAR, pltpu.SemaphoreType.REGULAR, dma((4, 2, 2)), dma((4, 2, 2)), dma((4, 2)), dma((4, 2)), dma((tp - 1,)), dma((tp - 1,)),
        dma((2, chunks)), dma((2, chunks)), dma((3, 4)), dma((3, 4)), dma((tp - 1,)), dma((tp - 1,)),
        dma((chunks, 4)), dma((chunks, 4)), dma((tp - 1,)), dma((tp - 1,)),
        dma((8,)), dma((tp - 1,)), dma((tp - 1,)), dma((chunks, tp - 1)), dma((chunks, tp - 1)), dma((tp - 1,)), dma((tp - 1,)), dma((3,)), dma((tp - 1,)),
    ]
    return pl.pallas_call(
        functools.partial(chain_kernel, stages, tp, chunk, head_dim),
        out_shape=outs,
        in_specs=[ANY] * 6 + [VMEM],
        out_specs=[ANY] * 13 + [VMEM],
        scratch_shapes=scratch,
        compiler_params=pltpu.CompilerParams(collective_id=0, has_side_effects=True, vmem_limit_bytes=67043328),
        name="chain",
    )(x_flat, dy_flat, wq, wo, w1, w2, params)


def wgrad_kernel(act, dy, gpre, h_two, gqkv, h_one, mix, gmid, h_all, gin_all, small,
                 gw_two, gw_one, gw_qkv, gw_out, h_out, g_in, g_ln, gb_out, gb_two, gb_one, gb_qkv,
                 act_v, dy_v, gpre_v, h_two_v, gq_v, h_one_v, mix_v, gmid_v, h_v, gin_v, two_v, one_v, qkv_v, out_v,
                 in_sem, two_sem, one_sem, qkv_sem, res_sem, keep_sem):
    heads, head_dim = gb_qkv.shape[1:]
    group = heads * head_dim
    pairs = ((act, act_v), (dy, dy_v), (gpre, gpre_v), (h_two, h_two_v), (gqkv, gq_v), (h_one, h_one_v), (mix, mix_v), (gmid, gmid_v), (h_all, h_v), (gin_all, gin_v))
    loads = [pltpu.make_async_copy(src, dst, in_sem.at[idx]) for idx, (src, dst) in enumerate(pairs)]
    for load in loads:
        load.start()
    g_ln[...] = small[0:4, :]
    gb_out[...] = small[4:5, :]
    gb_two[...] = small[5:6, :]
    gb_one[...] = small[6:7, :]

    def product(lhs, rhs, buf, dst, sem):
        def copy_of(row):
            rows = pl.ds(pl.multiple_of(row * group, group), group)
            return pltpu.make_async_copy(buf.at[rows], dst.at[rows], sem.at[row])

        @pl.loop(0, buf.shape[0] // group)
        def _(row):
            cols = pl.ds(pl.multiple_of(row * group, group), group)
            buf[cols, :] = dot_tn(lhs(row, cols), rhs[...])
            copy_of(row).start()

        return lambda: [copy_of(row).wait() for row in range(buf.shape[0] // group)]

    loads[0].wait()
    loads[1].wait()
    ends = [product(lambda row, cols: act_v[:, cols], dy_v, two_v, gw_two, two_sem)]
    loads[2].wait()
    loads[3].wait()
    ends.append(product(lambda row, cols: h_two_v[:, cols], gpre_v, one_v, gw_one, one_sem))
    loads[4].wait()
    loads[5].wait()
    ends.append(product(lambda row, cols: gq_v[:, cols], h_one_v, qkv_v, gw_qkv, qkv_sem))
    for part in range(3):
        total = jnp.sum(gq_v[:, part * group:(part + 1) * group].astype(F32), axis=0, keepdims=True)
        for h_idx in range(heads):
            gb_qkv[part, h_idx:h_idx + 1, :] = total[:, h_idx * head_dim:(h_idx + 1) * head_dim]
    loads[8].wait()
    loads[9].wait()
    keeps = [pltpu.make_async_copy(h_v, h_out, keep_sem.at[0]), pltpu.make_async_copy(gin_v, g_in, keep_sem.at[1])]
    for keep in keeps:
        keep.start()
    loads[6].wait()
    loads[7].wait()
    ends.append(product(lambda row, cols: mix_v[:, cols], gmid_v, out_v, gw_out, res_sem))
    for end in ends:
        end()
    for keep in keeps:
        keep.wait()


def run_wgrad(act, dy, gpre, h_two, gqkv, h_one, mix, gmid, h_all, gin_all, small, head_dim):
    def flat(array):
        return array.reshape(array.shape[0] * array.shape[1], array.shape[2])

    group, d_model, ff_local = mix.shape[2], dy.shape[2], act.shape[2]
    seqs, seq_len = dy.shape[:2]
    total = seqs * seq_len
    dma = pltpu.SemaphoreType.DMA
    grads = [(ff_local, d_model), (d_model, ff_local), (3 * group, d_model), (group, d_model)]
    rows = jax.ShapeDtypeStruct((total, d_model), BF16)
    smalls = [(4, d_model), (1, d_model), (1, d_model), (1, ff_local), (3, group // head_dim, head_dim)]
    widths = (ff_local, d_model, ff_local, d_model)
    return pl.pallas_call(
        wgrad_kernel,
        in_specs=[ANY] * 10 + [VMEM],
        out_specs=[ANY] * 6 + [VMEM] * 5,
        out_shape=[jax.ShapeDtypeStruct(shape, F32) for shape in grads] + [rows, rows] + [jax.ShapeDtypeStruct(shape, F32) for shape in smalls],
        scratch_shapes=[pltpu.VMEM((total, width), BF16) for width in widths]
        + [pltpu.VMEM((total, 3 * group), BF16), pltpu.VMEM((total, d_model), BF16), pltpu.VMEM((total, group), BF16)]
        + [pltpu.VMEM((total, d_model), BF16)] * 3 + [pltpu.VMEM(shape, F32) for shape in grads]
        + [dma((10,))] + [dma((shape[0] // group,)) for shape in grads] + [dma((2,))],
        compiler_params=pltpu.CompilerParams(vmem_limit_bytes=67043328),
        name="wgrad",
    )(flat(act), flat(dy), flat(gpre), flat(h_two), flat(gqkv), flat(h_one), flat(mix), flat(gmid), flat(h_all), flat(gin_all), small)


def solution(mesh):
    stages = mesh.shape["pp"]
    tp = mesh.shape["tp"]

    def stage_program(x_in, dy_out, w_qkv, b_qkv, w_out, b_out, ln_par, w_fc1, b_fc1, w_fc2, b_fc2):
        micro_count, batch_rows, seq_len, d_model = x_in.shape
        head_dim = w_qkv.shape[4]
        group = w_qkv.shape[3] * head_dim
        heads = group // head_dim
        seqs = micro_count * batch_rows
        wq = jnp.transpose(w_qkv[0], (0, 2, 3, 1)).reshape(3 * group, d_model)
        wo = w_out[0].reshape(group, d_model)
        w1, w2 = w_fc1[0], w_fc2[0]
        b_row = jnp.pad(b_qkv.reshape(1, 3 * group), ((0, 0), (0, d_model - 3 * group)))
        gap = jnp.zeros((6, d_model), BF16)
        params = jnp.concatenate([b_fc1, b_row, gap, ln_par[0], b_out, b_fc2, gap[:2]], axis=0).astype(F32)
        x_flat = x_in.reshape(seqs, seq_len, d_model)
        dy_flat = dy_out.reshape(seqs, seq_len, d_model)
        h_all, _, gin_all, gmid_all, mix_all, gqkv_all, _, dy_all, h_one, h_two, act, gpre, _, small = run_chain(
            stages, tp, x_flat, dy_flat, wq, wo, w1, w2, params, head_dim)
        gw_two, gw_one, gw_qkv, gw_out, h_out, g_in, g_ln, gb_out, gb_two, gb_one, gb_qkv = run_wgrad(
            act, dy_all, gpre, h_two, gqkv_all, h_one, mix_all, gmid_all, h_all, gin_all, small, head_dim)
        gw_qkv = jnp.transpose(gw_qkv.reshape(3, heads, head_dim, d_model), (0, 3, 1, 2))
        shape = (1, micro_count, batch_rows, seq_len, d_model)
        return (h_out.reshape(shape), g_in.reshape(shape), gw_qkv[None], gb_qkv[None], gw_out.reshape(1, heads, head_dim, d_model), gb_out,
                g_ln[None], gw_one[None], gb_one, gw_two[None], gb_two)

    act_spec = P(None, "dp", None, None)
    arg_specs = (act_spec, act_spec,
                 P("pp", None, None, "tp", None), P("pp", None, "tp", None), P("pp", "tp", None, None),
                 P("pp", None), P("pp", None, None), P("pp", None, "tp"), P("pp", "tp"),
                 P("pp", "tp", None), P("pp", None))
    stage_spec = P("pp", None, "dp", None, None)
    grad_axes = ("dp", "pp")
    result_specs = (stage_spec, stage_spec,
                    P(grad_axes, None, None, "tp", None), P(grad_axes, None, "tp", None), P(grad_axes, "tp", None, None),
                    P(grad_axes, None), P(grad_axes, None, None), P(grad_axes, None, "tp"), P(grad_axes, "tp"),
                    P(grad_axes, "tp", None), P(grad_axes, None))
    return jax.shard_map(stage_program, mesh=mesh, in_specs=arg_specs, out_specs=result_specs, check_vma=False)
```

time: 636 us -> 472 us (0.74)
  the two profiles are of different devices: /device:TPU:96 before, /device:TPU:97 now
where the time goes in v2:
time: 472 us; the launch traced here: 467 us
  Pallas kernels  464 us (98%)
    pallas_call x1, Pallas kernels, run_chain(): pl.pallas_call(functools.partial(chain_kernel, stages, tp, chunk, head_di...  444 us
    pallas_call x1, Pallas kernels, run_wgrad(): pl.pallas_call(wgrad_kernel, in_specs=[ANY] * 10 + [VMEM], out_specs=[ANY...  19.2 us

profile of v2, /device:TPU:97, one launch (start us, length us, event | category | flops | bytes accessed | tf_op | source)
XLA Modules:
  0.0 467.4 jit_solution(5685790409667430701)
XLA Ops:
  0.6 0.8 reshape.79
  1.4 1.5 concatenate.3
  2.9 0.6 convert_element_type.5.params
  3.5 444.4 %chain.1 = (bf16[4,384,1024]{2,1,0:T(8,128)(2,1)}, bf16[4,384,1024]{2,1,0:T(8,128)(2,1)}, bf16[4,384,1024]{2,1,0:T(8,128)(2,1)}, bf16[4,384,1024]{2,1,0:T(8,128)...) custom-call(bf16[4,384,1024]{2,1,0:T(8,128)(2,1)} %bitcast.33, ...), custom_call_target="tpu_custom_call" | custom-call | tf_op jit(solution)/shard_map/chain/pallas_call | solution.py:654
  448.0 19.2 %wgrad.1 = (f32[1024,1024]{1,0:T(8,128)}, f32[1024,1024]{1,0:T(8,128)}, f32[768,1024]{1,0:T(8,128)}, f32[256,1024]{1,0:T(8,128)}, bf16[1536,1024]{1,0:T(8,128)(2...) custom-call(bf16[1536,1024]{1,0:T(8,128)(2,1)} %bitcast.41, ...), custom_call_target="tpu_custom_call" | custom-call | tf_op jit(solution)/shard_map/wgrad/pallas_call | solution.py:732
  (3 shorter events, 0.0 us)

commit v3 on v2

--- a/solution.py
+++ b/solution.py
@@ -55,12 +55,13 @@
 
 
 def chain_kernel(stages, tp, chunk, head_dim,
-                 x_flat, dy_flat, wq_own, wo_own, w1_own, w2_own, params,
-                 h_all, mid_all, gin_all, gmid_all, mix_all, gqkv_all, x_all, dy_all, h_one_all, h_two_all, act_all, gpre_all, slope_all, small_out,
-                 wq, wq_t, wo, w1, w2, bias, x_buf, dy_buf, qkv, mix, mid, y_buf, gmid, gin, dkv, prob, dgelu, acc, hbuf, small,
+                 x_flat, dy_flat, wq_own, wo_own, w1_own, w2_own, ln_ref, b_qkv_ref, b_out_ref, b_one_ref, b_two_ref,
+                 h_all, mid_all, gin_all, gmid_all, mix_all, gqkv_all, x_all, dy_all, h_one_all, h_two_all, act_all, gpre_all, slope_all, land_one, land_two, land_gq, land_gm, small_out,
+                 wq, wq_t, wo, w1, w2, bias, x_buf, dy_buf, qkv, mix, mid, y_buf, gmid, gin, dkv, prob, dgelu, acc, hbuf, small, rep, bias_own,
                  own_sem, go_sem, done_sem, ring_send, ring_recv, fwd_send, fwd_recv, bias_send, bias_recv,
                  hop_send, hop_recv, ag_send, ag_recv, mix_send, mix_recv, bw_send, bw_recv, gq_send, gq_recv,
-                 out_sem, px_send, px_recv, py_send, py_recv, sum_send, sum_recv, prep_sem, post_sem):
+                 out_sem, px_send, px_recv, py_send, py_recv, sum_send, sum_recv, prep_sem, post_sem,
+                 lw_send, lw_recv, lf_send, lf_recv, lg_send, lg_recv):
     stage = lax.axis_index("pp")
     me = lax.axis_index("tp")
     seq_len, d_model = x_buf.shape
@@ -68,16 +69,31 @@
     group = wo_own.shape[0]
     heads = group // head_dim
     last = stages - 1
-    right, left = lax.rem(me + 1, tp), lax.rem(me + tp - 1, tp)
+    right, left, across = lax.rem(me + 1, tp), lax.rem(me + tp - 1, tp), lax.rem(me + 2, tp)
     not_first, not_last = stage > 0, stage < last
     peers = [lax.rem(me + off, tp) for off in range(1, tp)]
     even = lax.rem(stage, 2) == 0
     score_scale = head_dim ** -0.5
 
+    middle = stages // 2
+    eased, easing = stage == 1, stage == last
+    helped, helping = stage < 2, (stage >= middle) & (stage < middle + 2)
+    mate = lax.rem(stage + middle, stages)
+    far = jnp.where(eased, last, 1)
+
     def remote(src, dst, send, recv, axis, target):
         return pltpu.make_async_remote_copy(src_ref=src, dst_ref=dst, send_sem=send, recv_sem=recv,
                                             device_id={axis: target}, device_id_type=MESH)
 
+    bias_own[...] = jnp.zeros_like(bias_own)
+    bias_own[0:1, :] = b_one_ref[...].astype(F32)
+    for part in range(3):
+        for h_idx in range(heads):
+            col = part * group + h_idx * head_dim
+            bias_own[1:2, col:col + head_dim] = b_qkv_ref[part, h_idx:h_idx + 1, :].astype(F32)
+    rep[0:4, :] = ln_ref[...].astype(F32)
+    rep[4:5, :] = b_out_ref[...].astype(F32)
+    rep[5:6, :] = b_two_ref[...].astype(F32)
     small[...] = jnp.zeros_like(small)
     small_out[...] = jnp.zeros_like(small_out)
     barrier = pltpu.get_barrier_semaphore()
@@ -92,7 +108,18 @@
     def _():
         pl.semaphore_signal(barrier, inc=1, device_id={"pp": stage + 1}, device_id_type=MESH)
 
-    pl.semaphore_wait(barrier, tp - 1 + jnp.minimum(stage, 1) + jnp.minimum(last - stage, 1))
+    @pl.when(helped | helping)
+    def _():
+        for there in (me, across):
+            pl.semaphore_signal(barrier, inc=1, device_id={"pp": mate, "tp": there}, device_id_type=MESH)
+
+    @pl.when(eased | easing)
+    def _():
+        for there in (me, across):
+            pl.semaphore_signal(barrier, inc=1, device_id={"pp": far, "tp": there}, device_id_type=MESH)
+
+    near = tp - 1 + jnp.minimum(stage, 1) + jnp.minimum(last - stage, 1)
+    pl.semaphore_wait(barrier, near + jnp.where(helped | helping, 2, 0) + jnp.where(eased | easing, 2, 0))
 
     def shard(w_idx, origin):
         if w_idx == 1:
@@ -114,10 +141,27 @@
         return remote(block, block, fwd_send.at[w_idx, side], fwd_recv.at[w_idx, side], "tp", left if side else right)
 
     def bias_copy(slot):
-        return remote(params.at[pl.ds(0, 8)], bias.at[me], bias_send.at[slot], bias_recv.at[slot], "tp", peers[slot])
+        return remote(bias_own, bias.at[me], bias_send.at[slot], bias_recv.at[slot], "tp", peers[slot])
+
+    def detour(src, dst, send, recv, target, target_tp):
+        return pltpu.make_async_remote_copy(src_ref=src, dst_ref=dst, send_sem=send, recv_sem=recv,
+                                            device_id={"pp": target, "tp": target_tp}, device_id_type=MESH)
+
+    routes = ((2, 0, land_one, mate), (2, 1, land_one, far), (3, None, land_two, far))
+
+    def piece(ref, h_idx):
+        return ref if h_idx is None else half(ref, h_idx)
+
+    def lw_copy(idx):
+        w_idx, h_idx, land, target = routes[idx]
+        return detour(piece(owns[w_idx], h_idx), piece(land, h_idx), lw_send.at[idx], lw_recv.at[idx], target, across)
+
+    def lf_copy(idx):
+        w_idx, h_idx, land, target = routes[idx]
+        return detour(piece(land, h_idx), piece(shard(w_idx, across), h_idx), lf_send.at[idx], lf_recv.at[idx], target, me)
 
     own_copies = [pltpu.make_async_copy(owns[w_idx], shard(w_idx, me), own_sem.at[w_idx]) for w_idx in range(4)]
-    own_copies.append(pltpu.make_async_copy(params.at[pl.ds(0, 8)], bias.at[me], own_sem.at[4]))
+    own_copies.append(pltpu.make_async_copy(bias_own, bias.at[me], own_sem.at[4]))
     for own_copy in own_copies:
         own_copy.start()
     for slot in range(tp - 1):
@@ -137,6 +181,22 @@
         for copy in copies:
             copy.wait()
 
+    @pl.when(eased)
+    def _():
+        for idx in range(3):
+            lw_copy(idx).start()
+
+    @pl.when(stage == middle + 1)
+    def _():
+        lw_copy(0).wait_recv()
+        lf_copy(0).start()
+
+    @pl.when(easing)
+    def _():
+        for idx in (1, 2):
+            lw_copy(idx).wait_recv()
+            lf_copy(idx).start()
+
     @pl.when(jnp.logical_not(even))
     def _():
         pl.semaphore_wait(go_sem, 1)
@@ -158,10 +218,14 @@
     dkv[...] = jnp.zeros_like(dkv)
 
     for w_idx in range(4):
-        ring_copy(w_idx, 0, 0).wait_recv()
-        forward_copy(w_idx, 0).start()
-        ring_copy(w_idx, 1, 1).wait_recv()
-        forward_copy(w_idx, 1).start()
+        for side in range(2):
+            ring_copy(w_idx, side, side).wait_recv()
+            if w_idx < 2:
+                forward_copy(w_idx, side).start()
+            else:
+                @pl.when(jnp.logical_not(eased))
+                def _():
+                    forward_copy(w_idx, side).start()
     for own_copy in own_copies:
         own_copy.wait()
     for slot in range(tp - 1):
@@ -169,8 +233,9 @@
     for w_idx in range(4):
         ring_copy(w_idx, 1, 0).wait_recv()
         ring_copy(w_idx, 0, 1).wait_recv()
-        forward_copy(w_idx, 0).wait()
-        forward_copy(w_idx, 1).wait()
+        if w_idx < 2:
+            forward_copy(w_idx, 0).wait()
+            forward_copy(w_idx, 1).wait()
         for h_idx in range(2):
             ring_copy(w_idx, h_idx, 0).wait_send()
             ring_copy(w_idx, h_idx, 1).wait_send()
@@ -180,6 +245,27 @@
                 for part in range(3):
                     wq_t[t_idx, :, part * group:(part + 1) * group] = wq[t_idx, part * group:(part + 1) * group, :].T
 
+    @pl.when(jnp.logical_not(eased))
+    def _():
+        for w_idx in (2, 3):
+            forward_copy(w_idx, 0).wait()
+            forward_copy(w_idx, 1).wait()
+
+    @pl.when(eased)
+    def _():
+        for idx in range(3):
+            lf_copy(idx).wait_recv()
+            lw_copy(idx).wait_send()
+
+    @pl.when(stage == middle + 1)
+    def _():
+        lf_copy(0).wait_send()
+
+    @pl.when(easing)
+    def _():
+        for idx in (1, 2):
+            lf_copy(idx).wait_send()
+
     @pl.when(even)
     def _():
         pl.semaphore_signal(go_sem, inc=1, device_id={"pp": stage + 1}, device_id_type=MESH)
@@ -188,7 +274,6 @@
     def _():
         pl.semaphore_signal(done_sem, inc=1, device_id={"pp": stage - 1}, device_id_type=MESH)
 
-    rep = params.at[pl.ds(8, 8)]
     lane_head = lax.broadcasted_iota(jnp.int32, (chunk, group), 1) // head_dim
 
     def stack_heads(block):
@@ -291,11 +376,13 @@
         origin = peers[slot]
         return remote(h_all.at[origin], x_all.at[origin], px_send.at[slot], px_recv.at[slot], "pp", stage + 1)
 
-    def finish_fwd_gather():
+    def forward_fwd_gather():
         for kind in range(2):
             for side in range(2):
                 ag_copy(kind, side).wait_recv()
                 ag_forward(kind, side).start()
+
+    def finish_fwd_gather():
         for kind in range(2):
             for side in range(2):
                 ag_forward(kind, side).wait_recv()
@@ -336,6 +423,10 @@
         pl.semaphore_wait(done_sem, 1)
         start_fwd_gather()
 
+    @pl.when(stage < last - 1)
+    def _():
+        forward_fwd_gather()
+
     @pl.when(stage < stages // 2)
     def _():
         finish_fwd_gather()
@@ -354,6 +445,12 @@
 
     def gq_copy(slot):
         return remote(gqkv_of(peers[slot]), gqkv_all.at[me], gq_send.at[slot], gq_recv.at[slot], "tp", peers[slot])
+
+    def gl_copy(idx):
+        return detour(gmid if idx else gqkv_of(across), land_gm if idx else land_gq, lg_send.at[idx], lg_recv.at[idx], mate, across)
+
+    def gf_copy(idx):
+        return detour(land_gm if idx else land_gq, (gmid_all if idx else gqkv_all).at[across], lg_send.at[2 + idx], lg_recv.at[2 + idx], mate, me)
 
     def pass_dy(c_idx, slot):
         rows = pl.ds(c_idx * chunk, chunk)
@@ -519,23 +616,46 @@
     for out_copy in bwd_out:
         out_copy.start()
 
+    @pl.when(helped)
+    def _():
+        gl_copy(0).start()
+
+    @pl.when(stage == 0)
+    def _():
+        gl_copy(1).start()
+
+    @pl.when((stage >= stages // 2) & (stage < last - 1))
+    def _():
+        finish_fwd_gather()
+
     @pl.when(stage >= last - 1)
     def _():
+        forward_fwd_gather()
         forward_chunk(chunks - 1)
 
     for c_idx in range(chunks - 2, -1, -1):
         forward_chunk(c_idx)
 
-    @pl.when(stage >= stages // 2)
+    @pl.when(stage >= last - 1)
     def _():
         finish_fwd_gather()
 
     for side in range(2):
         ag_copy(2, side).start()
-    for slot in range(tp - 1):
-        gq_copy(slot).start()
-    for c_idx in range(chunks - 1, -1, -1):
-        pass_chunk(c_idx)
+    for slot in (0, 2, 1):
+        if slot == 1:
+            @pl.when(jnp.logical_not(helped))
+            def _():
+                gq_copy(slot).start()
+        else:
+            gq_copy(slot).start()
+    def pass_all():
+        for c_idx in range(chunks - 1, -1, -1):
+            pass_chunk(c_idx)
+
+    @pl.when(not_last)
+    def _():
+        pass_all()
 
     @pl.when(early)
     def _():
@@ -547,6 +667,10 @@
     def _():
         end_fwd_sends()
         prep(mid, x_buf, y_buf, False)
+
+    @pl.when(stage == last)
+    def _():
+        pass_all()
 
     def finish_rows(t_idx, src, dst, rows):
         grad = dot_nn(src[rows, :], w2_own_t[...]).astype(BF16).astype(F32) * dgelu[t_idx, rows, :]
@@ -560,9 +684,12 @@
     lax.fori_loop(0, chunks, finish_own, 0)
     own_keep = pltpu.make_async_copy(y_buf, gpre_all.at[me], prep_sem.at[0])
     own_keep.start()
-    for side in range(2):
-        ag_copy(2, side).wait_recv()
-        ag_forward(2, side).start()
+    @pl.when(not_first)
+    def _():
+        for side in range(2):
+            ag_copy(2, side).wait_recv()
+            ag_forward(2, side).start()
+
     own_keep.wait()
 
     def finish_peers(step, carry):
@@ -588,6 +715,17 @@
         return carry
 
     lax.fori_loop(0, chunks, finish_peers, 0)
+
+    @pl.when(helping)
+    def _():
+        gl_copy(0).wait_recv()
+        gf_copy(0).start()
+
+    @pl.when(stage == middle)
+    def _():
+        gl_copy(1).wait_recv()
+        gf_copy(1).start()
+
     for slot in range(tp - 1):
         sum_copy(slot).wait()
     total_small = small[0, 0:6, :]
@@ -597,12 +735,42 @@
 
     for slot in range(tp - 1):
         mix_copy(slot).wait_recv()
-        gq_copy(slot).wait()
+        if slot != 1:
+            gq_copy(slot).wait()
+
+    @pl.when(jnp.logical_not(helped))
+    def _():
+        gq_copy(1).wait()
+
+    @pl.when(not_first)
+    def _():
+        for side in range(2):
+            ag_forward(2, side).wait()
+
+    @pl.when(helped)
+    def _():
+        gl_copy(0).wait_send()
+        gf_copy(0).wait_recv()
+
+    @pl.when(stage == 0)
+    def _():
+        for side in range(2):
+            ag_copy(2, side).wait_recv()
+        gl_copy(1).wait_send()
+        gf_copy(1).wait_recv()
+
+    @pl.when(helping)
+    def _():
+        gf_copy(0).wait_send()
+
+    @pl.when(stage == middle)
+    def _():
+        gf_copy(1).wait_send()
+
     for side in range(2):
-        for kind in range(3):
+        for kind in range(2):
             ag_forward(kind, side).wait_send()
         ag_copy(2, side).wait_send()
-        ag_forward(2, side).wait_recv()
         for c_idx in range(chunks):
             bw_copy(c_idx, side).wait_send()
             bw_forward(c_idx, side).wait_send()
@@ -622,7 +790,7 @@
                 pass_dy(c_idx, slot).wait_send()
 
 
-def run_chain(stages, tp, x_flat, dy_flat, wq, wo, w1, w2, params, head_dim):
+def run_chain(stages, tp, x_flat, dy_flat, wq, wo, w1, w2, ln_par, b_qkv, b_out, b_one, b_two, head_dim):
     _, seq_len, d_model = x_flat.shape
     chunk = min(128, seq_len)
     chunks = seq_len // chunk
@@ -633,7 +801,8 @@
     outs = [jax.ShapeDtypeStruct(rows, BF16)] * 4
     outs += [jax.ShapeDtypeStruct((tp, seq_len, group), BF16), jax.ShapeDtypeStruct((tp, seq_len, 3 * group), BF16)]
     outs += [jax.ShapeDtypeStruct(rows, BF16)] * 4 + [jax.ShapeDtypeStruct((tp, seq_len, ff_local), BF16)] * 2
-    outs += [jax.ShapeDtypeStruct((tp, seq_len, ff_local), F32), jax.ShapeDtypeStruct((8, d_model), F32)]
+    outs += [jax.ShapeDtypeStruct((tp, seq_len, ff_local), F32), jax.ShapeDtypeStruct(w1.shape, BF16), jax.ShapeDtypeStruct(w2.shape, BF16)]
+    outs += [jax.ShapeDtypeStruct((seq_len, 3 * group), BF16), jax.ShapeDtypeStruct((seq_len, d_model), BF16), jax.ShapeDtypeStruct((8, d_model), F32)]
     act = pltpu.VMEM((seq_len, d_model), BF16)
     dma = pltpu.SemaphoreType.DMA
     scratch = [
@@ -646,20 +815,22 @@
         pltpu.VMEM((2, tp, seq_len, group), F32),
         pltpu.VMEM((chunks, tp, heads * chunk, seq_len), F32), pltpu.VMEM((tp, seq_len, ff_local), F32),
         pltpu.VMEM((chunk, d_model), F32), pltpu.VMEM((chunk, d_model), BF16), pltpu.VMEM((tp, 8, d_model), F32),
+        pltpu.VMEM((8, d_model), F32), pltpu.VMEM((8, d_model), F32),
         dma((9,)), pltpu.SemaphoreType.REGULAR, pltpu.SemaphoreType.REGULAR, dma((4, 2, 2)), dma((4, 2, 2)), dma((4, 2)), dma((4, 2)), dma((tp - 1,)), dma((tp - 1,)),
         dma((2, chunks)), dma((2, chunks)), dma((3, 4)), dma((3, 4)), dma((tp - 1,)), dma((tp - 1,)),
         dma((chunks, 4)), dma((chunks, 4)), dma((tp - 1,)), dma((tp - 1,)),
         dma((8,)), dma((tp - 1,)), dma((tp - 1,)), dma((chunks, tp - 1)), dma((chunks, tp - 1)), dma((tp - 1,)), dma((tp - 1,)), dma((3,)), dma((tp - 1,)),
+        dma((3,)), dma((3,)), dma((3,)), dma((3,)), dma((4,)), dma((4,)),
     ]
     return pl.pallas_call(
         functools.partial(chain_kernel, stages, tp, chunk, head_dim),
         out_shape=outs,
-        in_specs=[ANY] * 6 + [VMEM],
-        out_specs=[ANY] * 13 + [VMEM],
+        in_specs=[ANY] * 6 + [VMEM] * 5,
+        out_specs=[ANY] * 17 + [VMEM],
         scratch_shapes=scratch,
         compiler_params=pltpu.CompilerParams(collective_id=0, has_side_effects=True, vmem_limit_bytes=67043328),
         name="chain",
-    )(x_flat, dy_flat, wq, wo, w1, w2, params)
+    )(x_flat, dy_flat, wq, wo, w1, w2, ln_par, b_qkv, b_out, b_one, b_two)
 
 
 def wgrad_kernel(act, dy, gpre, h_two, gqkv, h_one, mix, gmid, h_all, gin_all, small,
@@ -677,28 +848,30 @@
     gb_two[...] = small[5:6, :]
     gb_one[...] = small[6:7, :]
 
-    def product(lhs, rhs, buf, dst, sem):
+    def product(lhs, rhs, buf, dst, sem, tiles):
+        tile = buf.shape[0] // tiles
+
         def copy_of(row):
-            rows = pl.ds(pl.multiple_of(row * group, group), group)
+            rows = pl.ds(pl.multiple_of(row * tile, tile), tile)
             return pltpu.make_async_copy(buf.at[rows], dst.at[rows], sem.at[row])
 
-        @pl.loop(0, buf.shape[0] // group)
+        @pl.loop(0, tiles)
         def _(row):
-            cols = pl.ds(pl.multiple_of(row * group, group), group)
-            buf[cols, :] = dot_tn(lhs(row, cols), rhs[...])
+            cols = pl.ds(pl.multiple_of(row * tile, tile), tile)
+            buf[cols, :] = dot_tn(lhs[:, cols], rhs[...])
             copy_of(row).start()
 
-        return lambda: [copy_of(row).wait() for row in range(buf.shape[0] // group)]
+        return lambda: [copy_of(row).wait() for row in range(tiles)]
 
     loads[0].wait()
     loads[1].wait()
-    ends = [product(lambda row, cols: act_v[:, cols], dy_v, two_v, gw_two, two_sem)]
+    ends = [product(act_v, dy_v, two_v, gw_two, two_sem, 2)]
     loads[2].wait()
     loads[3].wait()
-    ends.append(product(lambda row, cols: h_two_v[:, cols], gpre_v, one_v, gw_one, one_sem))
+    ends.append(product(h_two_v, gpre_v, one_v, gw_one, one_sem, 2))
     loads[4].wait()
     loads[5].wait()
-    ends.append(product(lambda row, cols: gq_v[:, cols], h_one_v, qkv_v, gw_qkv, qkv_sem))
+    ends.append(product(gq_v, h_one_v, qkv_v, gw_qkv, qkv_sem, 2))
     for part in range(3):
         total = jnp.sum(gq_v[:, part * group:(part + 1) * group].astype(F32), axis=0, keepdims=True)
         for h_idx in range(heads):
@@ -710,7 +883,7 @@
         keep.start()
     loads[6].wait()
     loads[7].wait()
-    ends.append(product(lambda row, cols: mix_v[:, cols], gmid_v, out_v, gw_out, res_sem))
+    ends.append(product(mix_v, gmid_v, out_v, gw_out, res_sem, 1))
     for end in ends:
         end()
     for keep in keeps:
@@ -756,13 +929,10 @@
         wq = jnp.transpose(w_qkv[0], (0, 2, 3, 1)).reshape(3 * group, d_model)
         wo = w_out[0].reshape(group, d_model)
         w1, w2 = w_fc1[0], w_fc2[0]
-        b_row = jnp.pad(b_qkv.reshape(1, 3 * group), ((0, 0), (0, d_model - 3 * group)))
-        gap = jnp.zeros((6, d_model), BF16)
-        params = jnp.concatenate([b_fc1, b_row, gap, ln_par[0], b_out, b_fc2, gap[:2]], axis=0).astype(F32)
         x_flat = x_in.reshape(seqs, seq_len, d_model)
         dy_flat = dy_out.reshape(seqs, seq_len, d_model)
-        h_all, _, gin_all, gmid_all, mix_all, gqkv_all, _, dy_all, h_one, h_two, act, gpre, _, small = run_chain(
-            stages, tp, x_flat, dy_flat, wq, wo, w1, w2, params, head_dim)
+        h_all, _, gin_all, gmid_all, mix_all, gqkv_all, _, dy_all, h_one, h_two, act, gpre, _, _, _, _, _, small = run_chain(
+            stages, tp, x_flat, dy_flat, wq, wo, w1, w2, ln_par[0], b_qkv[0], b_out, b_fc1, b_fc2, head_dim)
         gw_two, gw_one, gw_qkv, gw_out, h_out, g_in, g_ln, gb_out, gb_two, gb_one, gb_qkv = run_wgrad(
             act, dy_all, gpre, h_two, gqkv_all, h_one, mix_all, gmid_all, h_all, gin_all, small, head_dim)
         gw_qkv = jnp.transpose(gw_qkv.reshape(3, heads, head_dim, d_model), (0, 3, 1, 2))

time: 472 us -> 434 us (0.919)
  Pallas kernels: 464 us -> 432 us
    pallas_call x1, Pallas kernels: 444 us -> 414 us  [run_chain(): pl.pallas_call(functools.partial(chain_kernel, stages, tp, chunk, head_di...]
where the time goes in v3:
time: 434 us; the launch traced here: 433 us
  Pallas kernels  432 us (100%)
    pallas_call x1, Pallas kernels, run_chain(): pl.pallas_call(functools.partial(chain_kernel, stages, tp, chunk, head_di...  414 us
    pallas_call x1, Pallas kernels, run_wgrad(): pl.pallas_call(wgrad_kernel, in_specs=[ANY] * 10 + [VMEM], out_specs=[ANY...  18.1 us

profile of v3, /device:TPU:97, one launch (start us, length us, event | category | flops | bytes accessed | tf_op | source)
XLA Modules:
  0.0 433.1 jit_solution(10130582152679418326)
XLA Ops:
  0.6 414.2 %chain.1 = (bf16[4,384,1024]{2,1,0:T(8,128)(2,1)}, bf16[4,384,1024]{2,1,0:T(8,128)(2,1)}, bf16[4,384,1024]{2,1,0:T(8,128)(2,1)}, bf16[4,384,1024]{2,1,0:T(8,128)...) custom-call(bf16[4,384,1024]{2,1,0:T(8,128)(2,1)} %bitcast.34, ...), custom_call_target="tpu_custom_call" | custom-call | tf_op jit(solution)/shard_map/chain/pallas_call | solution.py:825
  414.8 18.1 %wgrad.1 = (f32[1024,1024]{1,0:T(8,128)}, f32[1024,1024]{1,0:T(8,128)}, f32[768,1024]{1,0:T(8,128)}, f32[256,1024]{1,0:T(8,128)}, bf16[1536,1024]{1,0:T(8,128)(2...) custom-call(bf16[1536,1024]{1,0:T(8,128)(2,1)} %bitcast.42, ...), custom_call_target="tpu_custom_call" | custom-call | tf_op jit(solution)/shard_map/wgrad/pallas_call | solution.py:905

commit v4 on v3

--- a/solution.py
+++ b/solution.py
@@ -56,10 +56,10 @@
 
 def chain_kernel(stages, tp, chunk, head_dim,
                  x_flat, dy_flat, wq_own, wo_own, w1_own, w2_own, ln_ref, b_qkv_ref, b_out_ref, b_one_ref, b_two_ref,
-                 h_all, mid_all, gin_all, gmid_all, mix_all, gqkv_all, x_all, dy_all, h_one_all, h_two_all, act_all, gpre_all, slope_all, land_one, land_two, land_gq, land_gm, small_out,
-                 wq, wq_t, wo, w1, w2, bias, x_buf, dy_buf, qkv, mix, mid, y_buf, gmid, gin, dkv, prob, dgelu, acc, hbuf, small, rep, bias_own,
+                 h_all, mid_all, gin_all, gmid_all, mix_all, gqkv_all, x_all, dy_all, h_one_all, h_two_all, act_all, gpre_all, slope_all, land_one, land_two, land_out, land_gq, land_gm, small_out,
+                 wq, wq_t, wo, w1, w2, bias, x_buf, dy_buf, qkv, mix, mid, y_buf, gmid, gin, dkv, prob, dgelu, acc, hbuf, small, rep, bias_own, gscore,
                  own_sem, go_sem, done_sem, ring_send, ring_recv, fwd_send, fwd_recv, bias_send, bias_recv,
-                 hop_send, hop_recv, ag_send, ag_recv, mix_send, mix_recv, bw_send, bw_recv, gq_send, gq_recv,
+                 hop_send, hop_recv, gm_send, gm_recv, mix_send, mix_recv, row_send, row_recv, gq_send, gq_recv,
                  out_sem, px_send, px_recv, py_send, py_recv, sum_send, sum_recv, prep_sem, post_sem,
                  lw_send, lw_recv, lf_send, lf_recv, lg_send, lg_recv):
     stage = lax.axis_index("pp")
@@ -80,6 +80,7 @@
     helped, helping = stage < 2, (stage >= middle) & (stage < middle + 2)
     mate = lax.rem(stage + middle, stages)
     far = jnp.where(eased, last, 1)
+    third, thirding = stage == middle - 1, stage == last
 
     def remote(src, dst, send, recv, axis, target):
         return pltpu.make_async_remote_copy(src_ref=src, dst_ref=dst, send_sem=send, recv_sem=recv,
@@ -118,8 +119,13 @@
         for there in (me, across):
             pl.semaphore_signal(barrier, inc=1, device_id={"pp": far, "tp": there}, device_id_type=MESH)
 
+    @pl.when(third | thirding)
+    def _():
+        for there in (me, across):
+            pl.semaphore_signal(barrier, inc=1, device_id={"pp": mate, "tp": there}, device_id_type=MESH)
+
     near = tp - 1 + jnp.minimum(stage, 1) + jnp.minimum(last - stage, 1)
-    pl.semaphore_wait(barrier, near + jnp.where(helped | helping, 2, 0) + jnp.where(eased | easing, 2, 0))
+    pl.semaphore_wait(barrier, near + jnp.where(helped | helping, 2, 0) + jnp.where(eased | easing, 2, 0) + jnp.where(third | thirding, 2, 0))
 
     def shard(w_idx, origin):
         if w_idx == 1:
@@ -147,7 +153,7 @@
         return pltpu.make_async_remote_copy(src_ref=src, dst_ref=dst, send_sem=send, recv_sem=recv,
                                             device_id={"pp": target, "tp": target_tp}, device_id_type=MESH)
 
-    routes = ((2, 0, land_one, mate), (2, 1, land_one, far), (3, None, land_two, far))
+    routes = ((2, 0, land_one, mate), (2, 1, land_one, far), (3, None, land_two, far), (1, None, land_out, mate))
 
     def piece(ref, h_idx):
         return ref if h_idx is None else half(ref, h_idx)
@@ -183,17 +189,22 @@
 
     @pl.when(eased)
     def _():
-        for idx in range(3):
+        for idx in range(4):
             lw_copy(idx).start()
 
+    @pl.when(third)
+    def _():
+        lw_copy(3).start()
+
     @pl.when(stage == middle + 1)
     def _():
-        lw_copy(0).wait_recv()
-        lf_copy(0).start()
+        for idx in (0, 3):
+            lw_copy(idx).wait_recv()
+            lf_copy(idx).start()
 
     @pl.when(easing)
     def _():
-        for idx in (1, 2):
+        for idx in (1, 2, 3):
             lw_copy(idx).wait_recv()
             lf_copy(idx).start()
 
@@ -220,12 +231,16 @@
     for w_idx in range(4):
         for side in range(2):
             ring_copy(w_idx, side, side).wait_recv()
-            if w_idx < 2:
+            if w_idx == 0:
                 forward_copy(w_idx, side).start()
             else:
-                @pl.when(jnp.logical_not(eased))
+                @pl.when(jnp.logical_not(eased | third) if w_idx == 1 else jnp.logical_not(eased))
                 def _():
                     forward_copy(w_idx, side).start()
+    @pl.when(even)
+    def _():
+        pl.semaphore_signal(go_sem, inc=1, device_id={"pp": stage + 1}, device_id_type=MESH)
+
     for own_copy in own_copies:
         own_copy.wait()
     for slot in range(tp - 1):
@@ -233,42 +248,48 @@
     for w_idx in range(4):
         ring_copy(w_idx, 1, 0).wait_recv()
         ring_copy(w_idx, 0, 1).wait_recv()
-        if w_idx < 2:
-            forward_copy(w_idx, 0).wait()
-            forward_copy(w_idx, 1).wait()
         for h_idx in range(2):
             ring_copy(w_idx, h_idx, 0).wait_send()
             ring_copy(w_idx, h_idx, 1).wait_send()
-        if w_idx == 0:
-            @pl.loop(0, tp)
-            def _(t_idx):
-                for part in range(3):
-                    wq_t[t_idx, :, part * group:(part + 1) * group] = wq[t_idx, part * group:(part + 1) * group, :].T
+    for side in range(2):
+        forward_copy(0, side).wait()
+
+    @pl.loop(0, tp)
+    def _(t_idx):
+        for part in range(3):
+            wq_t[t_idx, :, part * group:(part + 1) * group] = wq[t_idx, part * group:(part + 1) * group, :].T
 
     @pl.when(jnp.logical_not(eased))
     def _():
         for w_idx in (2, 3):
-            forward_copy(w_idx, 0).wait()
-            forward_copy(w_idx, 1).wait()
+            for side in range(2):
+                forward_copy(w_idx, side).wait()
+
+    @pl.when(jnp.logical_not(eased | third))
+    def _():
+        for side in range(2):
+            forward_copy(1, side).wait()
 
     @pl.when(eased)
     def _():
-        for idx in range(3):
+        for idx in range(4):
             lf_copy(idx).wait_recv()
             lw_copy(idx).wait_send()
 
+    @pl.when(third)
+    def _():
+        lf_copy(3).wait_recv()
+        lw_copy(3).wait_send()
+
     @pl.when(stage == middle + 1)
     def _():
-        lf_copy(0).wait_send()
+        for idx in (0, 3):
+            lf_copy(idx).wait_send()
 
     @pl.when(easing)
     def _():
-        for idx in (1, 2):
+        for idx in (1, 2, 3):
             lf_copy(idx).wait_send()
-
-    @pl.when(even)
-    def _():
-        pl.semaphore_signal(go_sem, inc=1, device_id={"pp": stage + 1}, device_id_type=MESH)
 
     @pl.when(jnp.logical_not(even))
     def _():
@@ -291,13 +312,32 @@
         src, dst, way, target = (y_buf, x_buf, 0, stage + 1) if forward else (gin, dy_buf, 1, stage - 1)
         return remote(src.at[rows], dst.at[rows], hop_send.at[way, c_idx], hop_recv.at[way, c_idx], "pp", target)
 
-    def fwd_chunk(c_idx, carry):
-        rows = pl.ds(pl.multiple_of(c_idx * chunk, chunk), chunk)
-
-        @pl.when(not_first)
-        def _():
-            hop_copy(c_idx, True).wait_recv()
-
+    size = group
+
+    def flip(ref_get, ref_set, count):
+        for row in range(count):
+            ref_set(row, row, ref_get(row, row).T)
+            for col in range(row):
+                upper, lower = ref_get(col, row).T, ref_get(row, col).T
+                ref_set(row, col, upper)
+                ref_set(col, row, lower)
+
+    def tile(row, col):
+        return slice(row * size, (row + 1) * size), slice(col * size, (col + 1) * size)
+
+    def flip_ff(ref, t_idx):
+        def ref_set(row, col, value):
+            ref[(t_idx,) + tile(row, col)] = value
+
+        flip(lambda row, col: ref[(t_idx,) + tile(row, col)], ref_set, d_model // size)
+
+    def flip_wo():
+        def ref_set(row, col, value):
+            wo[tile(row, col)] = value
+
+        flip(lambda row, col: wo[tile(row, col)], ref_set, d_model // size)
+
+    def layer_rows(c_idx, rows, flipping):
         normed, _ = norm_stats(x_buf[rows, :].astype(F32))
         hbuf[...] = (normed * rep[0:1, :] + rep[1:2, :]).astype(BF16)
 
@@ -323,6 +363,8 @@
         full_mix = jnp.concatenate([mix[t_idx, rows, :] for t_idx in groups], axis=1)
         x_mid = (x_buf[rows, :].astype(F32) + dot_nn(full_mix, wo[...]) + rep[4:5, :]).astype(BF16)
         mid[rows, :] = x_mid
+        if flipping:
+            flip_wo()
         normed_two, _ = norm_stats(x_mid.astype(F32))
         hbuf[...] = (normed_two * rep[2:3, :] + rep[3:4, :]).astype(BF16)
         total = jnp.zeros((chunk, d_model), F32)
@@ -331,40 +373,68 @@
             cdf, slope = gelu_parts(pre)
             dgelu[t_idx, rows, :] = slope
             total = total + dot_nn((pre * cdf).astype(BF16), w2[t_idx])
+            if flipping:
+                flip_ff(w1, t_idx)
 
         y_buf[rows, :] = (mid[rows, :].astype(F32) + total + rep[5:6, :]).astype(BF16)
 
+    gathers = ((y_buf, h_all), (mid, mid_all), (gin, gin_all))
+
+    def row_copy(kind, c_idx, side):
+        rows = pl.ds(c_idx * chunk, chunk)
+        src, dst = gathers[kind]
+        return remote(src.at[rows], dst.at[me, rows], row_send.at[kind, c_idx, side], row_recv.at[kind, c_idx, side], "tp", left if side else right)
+
+    def row_forward(kind, c_idx, side):
+        rows = pl.ds(c_idx * chunk + side * (chunk // 2), chunk // 2)
+        block = gathers[kind][1].at[right if side else left, rows]
+        return remote(block, block, row_send.at[kind, c_idx, 2 + side], row_recv.at[kind, c_idx, 2 + side], "tp", left if side else right)
+
+    def start_rows(c_idx):
+        for kind in range(2):
+            for side in range(2):
+                row_copy(kind, c_idx, side).start()
+
+    prompt = (stage >= middle) | jnp.logical_not(even)
+
+    def fwd_chunk(c_idx, carry):
+        rows = pl.ds(pl.multiple_of(c_idx * chunk, chunk), chunk)
+
+        @pl.when(not_first)
+        def _():
+            hop_copy(c_idx, True).wait_recv()
+
+        turning = (stage == last) & (c_idx == chunks - 1)
+
+        @pl.when(jnp.logical_not(turning))
+        def _():
+            layer_rows(c_idx, rows, False)
+
+        @pl.when(turning)
+        def _():
+            layer_rows(c_idx, rows, True)
+
         @pl.when(not_last)
         def _():
             hop_copy(c_idx, True).start()
 
+        @pl.when(prompt & even & (c_idx == 0))
+        def _():
+            pl.semaphore_wait(done_sem, 1)
+
+        @pl.when(prompt)
+        def _():
+            start_rows(c_idx)
+
         return carry
 
     lax.fori_loop(0, chunks, fwd_chunk, 0)
-
-    def ag_copy(kind, side):
-        src, dst = ((y_buf, h_all), (mid, mid_all), (gmid, gmid_all))[kind]
-        return remote(src, dst.at[me], ag_send.at[kind, side], ag_recv.at[kind, side], "tp", left if side else right)
-
-    def ag_forward(kind, side):
-        rows = pl.ds(side * (seq_len // 2), seq_len // 2)
-        block = (h_all, mid_all, gmid_all)[kind].at[right if side else left, rows]
-        return remote(block, block, ag_send.at[kind, 2 + side], ag_recv.at[kind, 2 + side], "tp", left if side else right)
 
     def mix_copy(slot):
         return remote(mix.at[peers[slot]], mix_all.at[me], mix_send.at[slot], mix_recv.at[slot], "tp", peers[slot])
 
-    def start_fwd_gather():
-        for kind in range(2):
-            for side in range(2):
-                ag_copy(kind, side).start()
-        for slot in range(tp - 1):
-            mix_copy(slot).start()
-
-    @pl.when(jnp.logical_not(even))
-    def _():
-        start_fwd_gather()
-
+    for slot in range(tp - 1):
+        mix_copy(slot).start()
     fwd_out = [pltpu.make_async_copy(y_buf, h_all.at[me], out_sem.at[0]),
                pltpu.make_async_copy(mid, mid_all.at[me], out_sem.at[1]),
                pltpu.make_async_copy(mix.at[me], mix_all.at[me], out_sem.at[2]),
@@ -377,51 +447,40 @@
         return remote(h_all.at[origin], x_all.at[origin], px_send.at[slot], px_recv.at[slot], "pp", stage + 1)
 
     def forward_fwd_gather():
-        for kind in range(2):
-            for side in range(2):
-                ag_copy(kind, side).wait_recv()
-                ag_forward(kind, side).start()
+        for c_idx in range(chunks):
+            for kind in range(2):
+                for side in range(2):
+                    row_copy(kind, c_idx, side).wait_recv()
+                    row_forward(kind, c_idx, side).start()
 
     def finish_fwd_gather():
-        for kind in range(2):
-            for side in range(2):
-                ag_forward(kind, side).wait_recv()
+        for c_idx in range(chunks):
+            for kind in range(2):
+                for side in range(2):
+                    row_forward(kind, c_idx, side).wait_recv()
 
         @pl.when(not_last)
         def _():
             for slot in range(tp - 1):
                 pass_x(slot).start()
 
-    size = group
-
-    def flip(ref_get, ref_set, count):
-        for row in range(count):
-            ref_set(row, row, ref_get(row, row).T)
-            for col in range(row):
-                upper, lower = ref_get(col, row).T, ref_get(row, col).T
-                ref_set(row, col, upper)
-                ref_set(col, row, lower)
-
-    def tile(row, col):
-        return slice(row * size, (row + 1) * size), slice(col * size, (col + 1) * size)
-
     @pl.loop(0, tp)
     def _(t_idx):
-        for ref in (w2, w1):
-            def ref_set(row, col, value, ref=ref):
-                ref[(t_idx,) + tile(row, col)] = value
-
-            flip(lambda row, col, ref=ref: ref[(t_idx,) + tile(row, col)], ref_set, d_model // size)
-
-    def wo_set(row, col, value):
-        wo[tile(row, col)] = value
-
-    flip(lambda row, col: wo[tile(row, col)], wo_set, d_model // size)
-
-    @pl.when(even)
+        flip_ff(w2, t_idx)
+
+    @pl.when(not_last)
+    def _():
+        @pl.loop(0, tp)
+        def _(t_idx):
+            flip_ff(w1, t_idx)
+
+        flip_wo()
+
+    @pl.when(jnp.logical_not(prompt))
     def _():
         pl.semaphore_wait(done_sem, 1)
-        start_fwd_gather()
+        for c_idx in range(chunks):
+            start_rows(c_idx)
 
     @pl.when(stage < last - 1)
     def _():
@@ -431,14 +490,13 @@
     def _():
         finish_fwd_gather()
 
-    def bw_copy(c_idx, side):
-        rows = pl.ds(c_idx * chunk, chunk)
-        return remote(gin.at[rows], gin_all.at[me, rows], bw_send.at[c_idx, side], bw_recv.at[c_idx, side], "tp", left if side else right)
-
-    def bw_forward(c_idx, side):
-        rows = pl.ds(c_idx * chunk + side * (chunk // 2), chunk // 2)
-        block = gin_all.at[right if side else left, rows]
-        return remote(block, block, bw_send.at[c_idx, 2 + side], bw_recv.at[c_idx, 2 + side], "tp", left if side else right)
+    def gm_copy(side):
+        return remote(gmid, gmid_all.at[me], gm_send.at[side], gm_recv.at[side], "tp", left if side else right)
+
+    def gm_forward(side):
+        rows = pl.ds(side * (seq_len // 2), seq_len // 2)
+        block = gmid_all.at[right if side else left, rows]
+        return remote(block, block, gm_send.at[2 + side], gm_recv.at[2 + side], "tp", left if side else right)
 
     def gqkv_of(t_idx):
         return wq_t.at[t_idx, pl.ds(0, seq_len)]
@@ -446,11 +504,14 @@
     def gq_copy(slot):
         return remote(gqkv_of(peers[slot]), gqkv_all.at[me], gq_send.at[slot], gq_recv.at[slot], "tp", peers[slot])
 
+    gm_way = jnp.where(eased | easing, far, mate)
+    gm_helping = (stage == middle) | easing
+
     def gl_copy(idx):
-        return detour(gmid if idx else gqkv_of(across), land_gm if idx else land_gq, lg_send.at[idx], lg_recv.at[idx], mate, across)
+        return detour(gmid if idx else gqkv_of(across), land_gm if idx else land_gq, lg_send.at[idx], lg_recv.at[idx], gm_way if idx else mate, across)
 
     def gf_copy(idx):
-        return detour(land_gm if idx else land_gq, (gmid_all if idx else gqkv_all).at[across], lg_send.at[2 + idx], lg_recv.at[2 + idx], mate, me)
+        return detour(land_gm if idx else land_gq, (gmid_all if idx else gqkv_all).at[across], lg_send.at[2 + idx], lg_recv.at[2 + idx], gm_way if idx else mate, me)
 
     def pass_dy(c_idx, slot):
         rows = pl.ds(c_idx * chunk, chunk)
@@ -459,12 +520,12 @@
 
     def forward_chunk(c_idx):
         for side in range(2):
-            bw_copy(c_idx, side).wait_recv()
-            bw_forward(c_idx, side).start()
+            row_copy(2, c_idx, side).wait_recv()
+            row_forward(2, c_idx, side).start()
 
     def pass_chunk(c_idx):
         for side in range(2):
-            bw_forward(c_idx, side).wait_recv()
+            row_forward(2, c_idx, side).wait_recv()
 
         @pl.when(not_first)
         def _():
@@ -523,9 +584,10 @@
         lax.fori_loop(0, tp, prep_seq, 0)
 
     def end_fwd_sends():
-        for kind in range(2):
-            for side in range(2):
-                ag_copy(kind, side).wait_send()
+        for c_idx in range(chunks):
+            for kind in range(2):
+                for side in range(2):
+                    row_copy(kind, c_idx, side).wait_send()
         for slot in range(tp - 1):
             mix_copy(slot).wait_send()
         for out_copy in fwd_out:
@@ -564,23 +626,21 @@
         small[me, 3:4, :] += g_shift
         small[me, 4:5, :] += jnp.sum(g_mid.astype(F32), axis=0, keepdims=True)
         small[me, 5:6, :] += jnp.sum(dy_wide, axis=0, keepdims=True)
-        g_mix_all = dot_nn(gmid[rows, :], wo[...]).astype(BF16)
-        g_stacks = [stack_heads(g_mix_all[:, t_idx * group:(t_idx + 1) * group]) for t_idx in groups]
+        hbuf[...] = dot_nn(gmid[rows, :], wo[...]).astype(BF16)
+        g_stacks = [stack_heads(hbuf[:, t_idx * group:(t_idx + 1) * group]) for t_idx in groups]
         g_probs = [dot_nt(g_stacks[t_idx], qkv[2, t_idx]).astype(BF16).astype(F32) for t_idx in groups]
-        g_values = [dot_tn(prob[c_idx, t_idx].astype(BF16), g_stacks[t_idx]) for t_idx in groups]
-        g_scores = []
+        g_values = [dot_tn(prob[c_idx, t_idx, :, rows].astype(BF16), g_stacks[t_idx]) for t_idx in groups]
         for t_idx in groups:
             probs = prob[c_idx, t_idx]
             inner = jnp.sum(g_probs[t_idx] * probs, axis=-1, keepdims=True)
-            g_scores.append((probs * (g_probs[t_idx] - inner)).astype(BF16))
-            dkv[1, t_idx] += g_values[t_idx]
+            gscore[t_idx] = (probs * (g_probs[t_idx] - inner)).astype(BF16)
+            wq_t[t_idx, rows, 2 * group:3 * group] = (dkv[1, t_idx, rows, :] + g_values[t_idx]).astype(BF16)
         for t_idx in groups:
-            wq_t[t_idx, rows, 0:group] = (unstack_heads(dot_nn(g_scores[t_idx], qkv[1, t_idx])) * score_scale).astype(BF16)
-            dkv[0, t_idx] += dot_tn(g_scores[t_idx], stack_heads(qkv[0, t_idx, rows, :])) * score_scale
+            wq_t[t_idx, rows, 0:group] = (unstack_heads(dot_nn(gscore[t_idx], qkv[1, t_idx])) * score_scale).astype(BF16)
+            g_keys = dot_tn(gscore[t_idx, :, rows], stack_heads(qkv[0, t_idx, rows, :]))
+            wq_t[t_idx, rows, group:2 * group] = ((dkv[0, t_idx, rows, :] + g_keys) * score_scale).astype(BF16)
         g_h_sum = jnp.zeros((chunk, d_model), F32)
         for t_idx in groups:
-            wq_t[t_idx, rows, group:2 * group] = dkv[0, t_idx, rows, :].astype(BF16)
-            wq_t[t_idx, rows, 2 * group:3 * group] = dkv[1, t_idx, rows, :].astype(BF16)
             g_h_sum = g_h_sum + dot_nn(wq_t[t_idx, rows, :], wq[t_idx])
 
         g_h_one = g_h_sum.astype(BF16).astype(F32)
@@ -594,7 +654,17 @@
             hop_copy(c_idx, False).start()
 
         for side in range(2):
-            bw_copy(c_idx, side).start()
+            row_copy(2, c_idx, side).start()
+
+        def earlier_rows(block, inner):
+            keys = pl.ds(pl.multiple_of(block * chunk, chunk), chunk)
+            for t_idx in groups:
+                dkv[0, t_idx, keys, :] += dot_tn(gscore[t_idx, :, keys], stack_heads(qkv[0, t_idx, rows, :]))
+                g_stack = stack_heads(hbuf[:, t_idx * group:(t_idx + 1) * group])
+                dkv[1, t_idx, keys, :] += dot_tn(prob[c_idx, t_idx, :, keys].astype(BF16), g_stack)
+            return inner
+
+        lax.fori_loop(0, c_idx, earlier_rows, 0)
 
         @pl.when((step >= 2) & (stage < last - 1))
         def _():
@@ -618,11 +688,9 @@
 
     @pl.when(helped)
     def _():
-        gl_copy(0).start()
-
-    @pl.when(stage == 0)
-    def _():
-        gl_copy(1).start()
+        for idx in range(2):
+            gl_copy(idx).start()
+
 
     @pl.when((stage >= stages // 2) & (stage < last - 1))
     def _():
@@ -641,7 +709,7 @@
         finish_fwd_gather()
 
     for side in range(2):
-        ag_copy(2, side).start()
+        gm_copy(side).start()
     for slot in (0, 2, 1):
         if slot == 1:
             @pl.when(jnp.logical_not(helped))
@@ -649,6 +717,7 @@
                 gq_copy(slot).start()
         else:
             gq_copy(slot).start()
+
     def pass_all():
         for c_idx in range(chunks - 1, -1, -1):
             pass_chunk(c_idx)
@@ -684,11 +753,21 @@
     lax.fori_loop(0, chunks, finish_own, 0)
     own_keep = pltpu.make_async_copy(y_buf, gpre_all.at[me], prep_sem.at[0])
     own_keep.start()
-    @pl.when(not_first)
+    @pl.when(helping)
+    def _():
+        gl_copy(0).wait_recv()
+        gf_copy(0).start()
+
+    @pl.when(gm_helping)
+    def _():
+        gl_copy(1).wait_recv()
+        gf_copy(1).start()
+
+    @pl.when(jnp.logical_not(helped))
     def _():
         for side in range(2):
-            ag_copy(2, side).wait_recv()
-            ag_forward(2, side).start()
+            gm_copy(side).wait_recv()
+            gm_forward(side).start()
 
     own_keep.wait()
 
@@ -715,17 +794,6 @@
         return carry
 
     lax.fori_loop(0, chunks, finish_peers, 0)
-
-    @pl.when(helping)
-    def _():
-        gl_copy(0).wait_recv()
-        gf_copy(0).start()
-
-    @pl.when(stage == middle)
-    def _():
-        gl_copy(1).wait_recv()
-        gf_copy(1).start()
-
     for slot in range(tp - 1):
         sum_copy(slot).wait()
     total_small = small[0, 0:6, :]
@@ -741,39 +809,32 @@
     @pl.when(jnp.logical_not(helped))
     def _():
         gq_copy(1).wait()
-
-    @pl.when(not_first)
-    def _():
         for side in range(2):
-            ag_forward(2, side).wait()
+            gm_forward(side).wait()
 
     @pl.when(helped)
     def _():
-        gl_copy(0).wait_send()
-        gf_copy(0).wait_recv()
-
-    @pl.when(stage == 0)
-    def _():
         for side in range(2):
-            ag_copy(2, side).wait_recv()
-        gl_copy(1).wait_send()
-        gf_copy(1).wait_recv()
+            gm_copy(side).wait_recv()
+        for idx in range(2):
+            gl_copy(idx).wait_send()
+            gf_copy(idx).wait_recv()
 
     @pl.when(helping)
     def _():
         gf_copy(0).wait_send()
 
-    @pl.when(stage == middle)
+    @pl.when(gm_helping)
     def _():
         gf_copy(1).wait_send()
 
     for side in range(2):
-        for kind in range(2):
-            ag_forward(kind, side).wait_send()
-        ag_copy(2, side).wait_send()
+        gm_copy(side).wait_send()
         for c_idx in range(chunks):
-            bw_copy(c_idx, side).wait_send()
-            bw_forward(c_idx, side).wait_send()
+            for kind in range(2):
+                row_forward(kind, c_idx, side).wait_send()
+            row_copy(2, c_idx, side).wait_send()
+            row_forward(2, c_idx, side).wait_send()
     for out_copy in bwd_out:
         out_copy.wait()
 
@@ -802,6 +863,7 @@
     outs += [jax.ShapeDtypeStruct((tp, seq_len, group), BF16), jax.ShapeDtypeStruct((tp, seq_len, 3 * group), BF16)]
     outs += [jax.ShapeDtypeStruct(rows, BF16)] * 4 + [jax.ShapeDtypeStruct((tp, seq_len, ff_local), BF16)] * 2
     outs += [jax.ShapeDtypeStruct((tp, seq_len, ff_local), F32), jax.ShapeDtypeStruct(w1.shape, BF16), jax.ShapeDtypeStruct(w2.shape, BF16)]
+    outs += [jax.ShapeDtypeStruct(wo.shape, BF16)]
     outs += [jax.ShapeDtypeStruct((seq_len, 3 * group), BF16), jax.ShapeDtypeStruct((seq_len, d_model), BF16), jax.ShapeDtypeStruct((8, d_model), F32)]
     act = pltpu.VMEM((seq_len, d_model), BF16)
     dma = pltpu.SemaphoreType.DMA
@@ -815,18 +877,18 @@
         pltpu.VMEM((2, tp, seq_len, group), F32),
         pltpu.VMEM((chunks, tp, heads * chunk, seq_len), F32), pltpu.VMEM((tp, seq_len, ff_local), F32),
         pltpu.VMEM((chunk, d_model), F32), pltpu.VMEM((chunk, d_model), BF16), pltpu.VMEM((tp, 8, d_model), F32),
-        pltpu.VMEM((8, d_model), F32), pltpu.VMEM((8, d_model), F32),
+        pltpu.VMEM((8, d_model), F32), pltpu.VMEM((8, d_model), F32), pltpu.VMEM((tp, heads * chunk, seq_len), BF16),
         dma((9,)), pltpu.SemaphoreType.REGULAR, pltpu.SemaphoreType.REGULAR, dma((4, 2, 2)), dma((4, 2, 2)), dma((4, 2)), dma((4, 2)), dma((tp - 1,)), dma((tp - 1,)),
-        dma((2, chunks)), dma((2, chunks)), dma((3, 4)), dma((3, 4)), dma((tp - 1,)), dma((tp - 1,)),
-        dma((chunks, 4)), dma((chunks, 4)), dma((tp - 1,)), dma((tp - 1,)),
+        dma((2, chunks)), dma((2, chunks)), dma((4,)), dma((4,)), dma((tp - 1,)), dma((tp - 1,)),
+        dma((3, chunks, 4)), dma((3, chunks, 4)), dma((tp - 1,)), dma((tp - 1,)),
         dma((8,)), dma((tp - 1,)), dma((tp - 1,)), dma((chunks, tp - 1)), dma((chunks, tp - 1)), dma((tp - 1,)), dma((tp - 1,)), dma((3,)), dma((tp - 1,)),
-        dma((3,)), dma((3,)), dma((3,)), dma((3,)), dma((4,)), dma((4,)),
+        dma((4,)), dma((4,)), dma((4,)), dma((4,)), dma((4,)), dma((4,)),
     ]
     return pl.pallas_call(
         functools.partial(chain_kernel, stages, tp, chunk, head_dim),
         out_shape=outs,
         in_specs=[ANY] * 6 + [VMEM] * 5,
-        out_specs=[ANY] * 17 + [VMEM],
+        out_specs=[ANY] * 18 + [VMEM],
         scratch_shapes=scratch,
         compiler_params=pltpu.CompilerParams(collective_id=0, has_side_effects=True, vmem_limit_bytes=67043328),
         name="chain",
@@ -931,7 +993,7 @@
         w1, w2 = w_fc1[0], w_fc2[0]
         x_flat = x_in.reshape(seqs, seq_len, d_model)
         dy_flat = dy_out.reshape(seqs, seq_len, d_model)
-        h_all, _, gin_all, gmid_all, mix_all, gqkv_all, _, dy_all, h_one, h_two, act, gpre, _, _, _, _, _, small = run_chain(
+        h_all, _, gin_all, gmid_all, mix_all, gqkv_all, _, dy_all, h_one, h_two, act, gpre, _, _, _, _, _, _, small = run_chain(
             stages, tp, x_flat, dy_flat, wq, wo, w1, w2, ln_par[0], b_qkv[0], b_out, b_fc1, b_fc2, head_dim)
         gw_two, gw_one, gw_qkv, gw_out, h_out, g_in, g_ln, gb_out, gb_two, gb_one, gb_qkv = run_wgrad(
             act, dy_all, gpre, h_two, gqkv_all, h_one, mix_all, gmid_all, h_all, gin_all, small, head_dim)

time: 434 us -> 431 us (level); the launches traced: 433 us -> 422 us
  Pallas kernels: 432 us -> 421 us
    pallas_call x1, Pallas kernels: 414 us -> 403 us  [run_chain(): pl.pallas_call(functools.partial(chain_kernel, stages, tp, chunk, head_di...]
where the time goes in v4:
time: 431 us; the launch traced here: 422 us
  Pallas kernels  421 us (98%)
    pallas_call x1, Pallas kernels, run_chain(): pl.pallas_call(functools.partial(chain_kernel, stages, tp, chunk, head_di...  403 us
    pallas_call x1, Pallas kernels, run_wgrad(): pl.pallas_call(wgrad_kernel, in_specs=[ANY] * 10 + [VMEM], out_specs=[ANY...  18.1 us

profile of v4, /device:TPU:97, one launch (start us, length us, event | category | flops | bytes accessed | tf_op | source)
XLA Modules:
  0.0 422.3 jit_solution(17647596786049622030)
XLA Ops:
  0.6 403.4 %chain.1 = (bf16[4,384,1024]{2,1,0:T(8,128)(2,1)}, bf16[4,384,1024]{2,1,0:T(8,128)(2,1)}, bf16[4,384,1024]{2,1,0:T(8,128)(2,1)}, bf16[4,384,1024]{2,1,0:T(8,128)...) custom-call(bf16[4,384,1024]{2,1,0:T(8,128)(2,1)} %bitcast.34, ...), custom_call_target="tpu_custom_call" | custom-call | tf_op jit(solution)/shard_map/chain/pallas_call | solution.py:887
  404.0 18.1 %wgrad.1 = (f32[1024,1024]{1,0:T(8,128)}, f32[1024,1024]{1,0:T(8,128)}, f32[768,1024]{1,0:T(8,128)}, f32[256,1024]{1,0:T(8,128)}, bf16[1536,1024]{1,0:T(8,128)(2...) custom-call(bf16[1536,1024]{1,0:T(8,128)(2,1)} %bitcast.42, ...), custom_call_target="tpu_custom_call" | custom-call | tf_op jit(solution)/shard_map/wgrad/pallas_call | solution.py:967

commit v5 on v4

--- a/solution.py
+++ b/solution.py
@@ -80,7 +80,6 @@
     helped, helping = stage < 2, (stage >= middle) & (stage < middle + 2)
     mate = lax.rem(stage + middle, stages)
     far = jnp.where(eased, last, 1)
-    third, thirding = stage == middle - 1, stage == last
 
     def remote(src, dst, send, recv, axis, target):
         return pltpu.make_async_remote_copy(src_ref=src, dst_ref=dst, send_sem=send, recv_sem=recv,
@@ -119,13 +118,8 @@
         for there in (me, across):
             pl.semaphore_signal(barrier, inc=1, device_id={"pp": far, "tp": there}, device_id_type=MESH)
 
-    @pl.when(third | thirding)
-    def _():
-        for there in (me, across):
-            pl.semaphore_signal(barrier, inc=1, device_id={"pp": mate, "tp": there}, device_id_type=MESH)
-
     near = tp - 1 + jnp.minimum(stage, 1) + jnp.minimum(last - stage, 1)
-    pl.semaphore_wait(barrier, near + jnp.where(helped | helping, 2, 0) + jnp.where(eased | easing, 2, 0) + jnp.where(third | thirding, 2, 0))
+    pl.semaphore_wait(barrier, near + jnp.where(helped | helping, 2, 0) + jnp.where(eased | easing, 2, 0))
 
     def shard(w_idx, origin):
         if w_idx == 1:
@@ -192,10 +186,6 @@
         for idx in range(4):
             lw_copy(idx).start()
 
-    @pl.when(third)
-    def _():
-        lw_copy(3).start()
-
     @pl.when(stage == middle + 1)
     def _():
         for idx in (0, 3):
@@ -204,7 +194,7 @@
 
     @pl.when(easing)
     def _():
-        for idx in (1, 2, 3):
+        for idx in (1, 2):
             lw_copy(idx).wait_recv()
             lf_copy(idx).start()
 
@@ -234,7 +224,7 @@
             if w_idx == 0:
                 forward_copy(w_idx, side).start()
             else:
-                @pl.when(jnp.logical_not(eased | third) if w_idx == 1 else jnp.logical_not(eased))
+                @pl.when(jnp.logical_not(eased))
                 def _():
                     forward_copy(w_idx, side).start()
     @pl.when(even)
@@ -261,14 +251,9 @@
 
     @pl.when(jnp.logical_not(eased))
     def _():
-        for w_idx in (2, 3):
+        for w_idx in (1, 2, 3):
             for side in range(2):
                 forward_copy(w_idx, side).wait()
-
-    @pl.when(jnp.logical_not(eased | third))
-    def _():
-        for side in range(2):
-            forward_copy(1, side).wait()
 
     @pl.when(eased)
     def _():
@@ -276,11 +261,6 @@
             lf_copy(idx).wait_recv()
             lw_copy(idx).wait_send()
 
-    @pl.when(third)
-    def _():
-        lf_copy(3).wait_recv()
-        lw_copy(3).wait_send()
-
     @pl.when(stage == middle + 1)
     def _():
         for idx in (0, 3):
@@ -288,7 +268,7 @@
 
     @pl.when(easing)
     def _():
-        for idx in (1, 2, 3):
+        for idx in (1, 2):
             lf_copy(idx).wait_send()
 
     @pl.when(jnp.logical_not(even))
@@ -931,6 +911,11 @@
     loads[2].wait()
     loads[3].wait()
     ends.append(product(h_two_v, gpre_v, one_v, gw_one, one_sem, 2))
+    loads[8].wait()
+    loads[9].wait()
+    keeps = [pltpu.make_async_copy(h_v, h_out, keep_sem.at[0]), pltpu.make_async_copy(gin_v, g_in, keep_sem.at[1])]
+    for keep in keeps:
+        keep.start()
     loads[4].wait()
     loads[5].wait()
     ends.append(product(gq_v, h_one_v, qkv_v, gw_qkv, qkv_sem, 2))
@@ -938,11 +923,6 @@
         total = jnp.sum(gq_v[:, part * group:(part + 1) * group].astype(F32), axis=0, keepdims=True)
         for h_idx in range(heads):
             gb_qkv[part, h_idx:h_idx + 1, :] = total[:, h_idx * head_dim:(h_idx + 1) * head_dim]
-    loads[8].wait()
-    loads[9].wait()
-    keeps = [pltpu.make_async_copy(h_v, h_out, keep_sem.at[0]), pltpu.make_async_copy(gin_v, g_in, keep_sem.at[1])]
-    for keep in keeps:
-        keep.start()
     loads[6].wait()
     loads[7].wait()
     ends.append(product(mix_v, gmid_v, out_v, gw_out, res_sem, 1))

time: 431 us -> 430 us (level)
  no operation moved by 1% of the time
where the time goes in v5:
time: 430 us; the launch traced here: 422 us
  Pallas kernels  421 us (98%)
    pallas_call x1, Pallas kernels, run_chain(): pl.pallas_call(functools.partial(chain_kernel, stages, tp, chunk, head_di...  403 us
    pallas_call x1, Pallas kernels, run_wgrad(): pl.pallas_call(wgrad_kernel, in_specs=[ANY] * 10 + [VMEM], out_specs=[ANY...  18.8 us

profile of v5, /device:TPU:97, one launch (start us, length us, event | category | flops | bytes accessed | tf_op | source)
XLA Modules:
  0.0 422.1 jit_solution(15355470160575102097)
XLA Ops:
  0.6 402.5 %chain.1 = (bf16[4,384,1024]{2,1,0:T(8,128)(2,1)}, bf16[4,384,1024]{2,1,0:T(8,128)(2,1)}, bf16[4,384,1024]{2,1,0:T(8,128)(2,1)}, bf16[4,384,1024]{2,1,0:T(8,128)...) custom-call(bf16[4,384,1024]{2,1,0:T(8,128)(2,1)} %bitcast.34, ...), custom_call_target="tpu_custom_call" | custom-call | tf_op jit(solution)/shard_map/chain/pallas_call | solution.py:867
  403.2 18.8 %wgrad.1 = (f32[1024,1024]{1,0:T(8,128)}, f32[1024,1024]{1,0:T(8,128)}, f32[768,1024]{1,0:T(8,128)}, f32[256,1024]{1,0:T(8,128)}, bf16[1536,1024]{1,0:T(8,128)(2...) custom-call(bf16[1536,1024]{1,0:T(8,128)(2,1)} %bitcast.42, ...), custom_call_target="tpu_custom_call" | custom-call | tf_op jit(solution)/shard_map/wgrad/pallas_call | solution.py:947
